TPU v7x, 8 devices: a whole 2x2x1 slice. The times are simulated.
8 devices in a mesh: terms: 8 (over z, y, x, core).
Axes of the slice: x: 2, y: 2, z: 1, core: 2. Of those that a mesh axis runs over, the one named last changes fastest.
Arguments:
- psi: float32 [2, 128, 4, 4, 128], replicated
- left_env: bfloat16 [128, 128, 128], P('terms')
- phys_op: bfloat16 [128, 16, 16], P('terms')
- right_env: bfloat16 [128, 128, 128], P('terms')
Outputs:
- output 1: float32 [2, 7, 128, 4, 4, 128], P(None, None, 'terms')
- output 2: float32 [2, 6], replicated
- output 3: float32 [2, 6], replicated
All inputs are finite; a program needn't handle non-finite values.
Results may differ from a plain program's by a relative error of at most 0.0107488.
Values are sent between devices in bfloat16 or wider.
A program may use at most 1 GiB of HBM per device.

v0:
```python
import jax
import jax.numpy as jnp
from jax import lax
from jax.sharding import PartitionSpec as P

LANCZOS_STEPS = 6


def solution(mesh):
    dev_count = mesh.shape['terms']

    def device_fn(psi, left_loc, phys_loc, right_loc):
        roots, bond_dim, phys_dim = psi.shape[0], psi.shape[1], psi.shape[2]
        pairs = phys_dim * phys_dim
        rows = bond_dim // dev_count
        n_elems = bond_dim * pairs * bond_dim
        psi_mat = psi.reshape(roots, bond_dim, pairs, bond_dim)
        norms = jnp.sqrt(jnp.sum(psi_mat * psi_mat, axis=(1, 2, 3)) / n_elems)
        v_full = psi_mat / norms[:, None, None, None]
        row_start = lax.axis_index('terms') * rows
        v_cur = lax.dynamic_slice_in_dim(v_full, row_start, rows, axis=1)
        v_in = v_full.astype(jnp.bfloat16)
        v_prev = jnp.zeros_like(v_cur)
        beta_prev = jnp.zeros((roots,), jnp.float32)
        vectors = [v_cur]
        alphas = []
        betas = []
        for step_idx in range(LANCZOS_STEPS):
            right_part = jnp.einsum('rcup,kbp->krcub', v_in, right_loc, preferred_element_type=jnp.float32).astype(jnp.bfloat16)
            mid_part = jnp.einsum('kqu,krcub->krcqb', phys_loc, right_part, preferred_element_type=jnp.float32).astype(jnp.bfloat16)
            part_sigma = jnp.einsum('kac,krcqb->raqb', left_loc, mid_part, preferred_element_type=jnp.float32)
            sigma = lax.psum_scatter(part_sigma, 'terms', scatter_dimension=1, tiled=True)
            alpha = lax.psum(jnp.sum(sigma * v_cur, axis=(1, 2, 3)), 'terms') / n_elems
            residual = sigma - alpha[:, None, None, None] * v_cur - beta_prev[:, None, None, None] * v_prev
            beta = jnp.sqrt(lax.psum(jnp.sum(residual * residual, axis=(1, 2, 3)), 'terms') / n_elems)
            v_next = residual / beta[:, None, None, None]
            if step_idx + 1 < LANCZOS_STEPS:
                v_in = lax.all_gather(v_next.astype(jnp.bfloat16), 'terms', axis=1, tiled=True)
            vectors.append(v_next)
            alphas.append(alpha)
            betas.append(beta)
            v_prev, v_cur, beta_prev = v_cur, v_next, beta
        stacked = jnp.stack(vectors, axis=1).reshape(roots, LANCZOS_STEPS + 1, rows, phys_dim, phys_dim, bond_dim)
        return stacked, jnp.stack(alphas, axis=1), jnp.stack(betas, axis=1)

    return jax.shard_map(device_fn, mesh=mesh, in_specs=(P(), P('terms'), P('terms'), P('terms')), out_specs=(P(None, None, 'terms'), P(), P()), check_vma=False)
```

profile of v0, /device:TPU:0, one launch (start us, length us, event | category | flops | bytes accessed | tf_op | source)
XLA Modules:
  0.0 903.8 jit_solution(17084491064637550610)
XLA Ops:
  20.3 19.9 %convert_bitcast_fusion.10 = bf16[16,2,128,16,128]{4,3,2,1,0:T(8,128)(2,1)} fusion(bf16[16,2,128,16,128]{4,2,0,3,1:T(8,128)(2,1)} %convert_bitcast_fusion.11, bf16[16,16,16]{2,1,0:T(8,128)(2,1)S(1)} %copy-done.1), kind=kOutput, calls=%fused_computation.34 | convolution fusion | flops 276824064 | bytes 33562624 | tf_op jit(solution)/shard_map/kqu,krcub->krcqb/dot_general | solution.py:30
  59.5 35.5 %reduce-scatter.7.cloned.1.call-done = f32[2,16,16,128]{3,2,0,1:T(8,128)} async-done(((f32[2,128,16,128]{3,2,0,1:T(8,128)}), f32[2,16,16,128]{3,2,0,1:T(8,128)}) %reduce-scatter.7.cloned.1.call-update) | async-done | bytes 262160 | tf_op jit(solution)/shard_map/reduce_scatter | solution.py:32
  96.2 22.2 %psum.84 = f32[2]{0:T(128)S(1)} all-reduce(f32[2]{0:T(128)S(1)} %get-tuple-element.32), channel_id=1, replica_groups=mesh['terms'=8] {'terms'}, use_global_device_ids=true, to_apply=%region_3.0 | all-reduce | flops 2 | bytes 16 | tf_op jit(solution)/shard_map/psum | solution.py:33
  119.6 23.9 %psum.85 = f32[2]{0:T(128)S(1)} all-reduce(f32[2]{0:T(128)S(1)} %multiply_reduce_fusion.11), channel_id=1, replica_groups=mesh['terms'=8] {'terms'}, use_global_device_ids=true, to_apply=%region_5.0 | all-reduce | flops 2 | bytes 16 | tf_op jit(solution)/shard_map/psum | solution.py:35
  173.5 19.8 %convert_bitcast_fusion.8 = bf16[16,2,128,16,128]{4,3,2,1,0:T(8,128)(2,1)} fusion(bf16[16,2,128,16,128]{4,2,0,3,1:T(8,128)(2,1)} %convert_bitcast_fusion.9, bf16[16,16,16]{2,1,0:T(8,128)(2,1)S(1)} %copy-done.1), kind=kOutput, calls=%fused_computation.32 | convolution fusion | flops 276824064 | bytes 33562624 | tf_op jit(solution)/shard_map/kqu,krcub->krcqb/dot_general | solution.py:30
  212.8 32.7 %reduce-scatter.9.cloned.1.call-done = f32[2,16,16,128]{3,2,0,1:T(8,128)} async-done(((f32[2,128,16,128]{3,2,0,1:T(8,128)}), f32[2,16,16,128]{3,2,0,1:T(8,128)}) %reduce-scatter.9.cloned.1.call-update) | async-done | bytes 262160 | tf_op jit(solution)/shard_map/reduce_scatter | solution.py:32
  246.7 22.2 %psum.86 = f32[2]{0:T(128)S(1)} all-reduce(f32[2]{0:T(128)S(1)} %multiply_reduce_fusion.10), channel_id=1, replica_groups=mesh['terms'=8] {'terms'}, use_global_device_ids=true, to_apply=%region_8.0 | all-reduce | flops 2 | bytes 16 | tf_op jit(solution)/shard_map/psum | solution.py:33
  270.1 23.9 %psum.87 = f32[2]{0:T(128)S(1)} all-reduce(f32[2]{0:T(128)S(1)} %get-tuple-element.28), channel_id=1, replica_groups=mesh['terms'=8] {'terms'}, use_global_device_ids=true, to_apply=%region_10.0 | all-reduce | flops 2 | bytes 16 | tf_op jit(solution)/shard_map/psum | solution.py:35
  322.9 19.8 %convert_bitcast_fusion.6 = bf16[16,2,128,16,128]{4,3,2,1,0:T(8,128)(2,1)} fusion(bf16[16,2,128,16,128]{4,2,0,3,1:T(8,128)(2,1)} %convert_bitcast_fusion.7, bf16[16,16,16]{2,1,0:T(8,128)(2,1)S(1)} %copy-done.1), kind=kOutput, calls=%fused_computation.30 | convolution fusion | flops 276824064 | bytes 33562624 | tf_op jit(solution)/shard_map/kqu,krcub->krcqb/dot_general | solution.py:30
  361.9 32.7 %reduce-scatter.11.cloned.1.call-done = f32[2,16,16,128]{3,2,0,1:T(8,128)} async-done(((f32[2,128,16,128]{3,2,0,1:T(8,128)}), f32[2,16,16,128]{3,2,0,1:T(8,128)}) %reduce-scatter.11.cloned.1.call-update) | async-done | bytes 262160 | tf_op jit(solution)/shard_map/reduce_scatter | solution.py:32
  395.8 22.2 %psum.88 = f32[2]{0:T(128)S(1)} all-reduce(f32[2]{0:T(128)S(1)} %multiply_reduce_fusion.8), channel_id=1, replica_groups=mesh['terms'=8] {'terms'}, use_global_device_ids=true, to_apply=%region_13.0 | all-reduce | flops 2 | bytes 16 | tf_op jit(solution)/shard_map/psum | solution.py:33
  419.2 23.9 %psum.89 = f32[2]{0:T(128)S(1)} all-reduce(f32[2]{0:T(128)S(1)} %get-tuple-element.24), channel_id=1, replica_groups=mesh['terms'=8] {'terms'}, use_global_device_ids=true, to_apply=%region_15.0 | all-reduce | flops 2 | bytes 16 | tf_op jit(solution)/shard_map/psum | solution.py:35
  472.0 19.8 %convert_bitcast_fusion.4 = bf16[16,2,128,16,128]{4,3,2,1,0:T(8,128)(2,1)} fusion(bf16[16,2,128,16,128]{4,2,0,3,1:T(8,128)(2,1)} %convert_bitcast_fusion.5, bf16[16,16,16]{2,1,0:T(8,128)(2,1)S(1)} %copy-done.1), kind=kOutput, calls=%fused_computation.28 | convolution fusion | flops 276824064 | bytes 33562624 | tf_op jit(solution)/shard_map/kqu,krcub->krcqb/dot_general | solution.py:30
  511.3 32.7 %reduce-scatter.13.cloned.1.call-done = f32[2,16,16,128]{3,2,0,1:T(8,128)} async-done(((f32[2,128,16,128]{3,2,0,1:T(8,128)}), f32[2,16,16,128]{3,2,0,1:T(8,128)}) %reduce-scatter.13.cloned.1.call-update) | async-done | bytes 262160 | tf_op jit(solution)/shard_map/reduce_scatter | solution.py:32
  545.2 22.2 %psum.90 = f32[2]{0:T(128)S(1)} all-reduce(f32[2]{0:T(128)S(1)} %multiply_reduce_fusion.6), channel_id=1, replica_groups=mesh['terms'=8] {'terms'}, use_global_device_ids=true, to_apply=%region_18.0 | all-reduce | flops 2 | bytes 16 | tf_op jit(solution)/shard_map/psum | solution.py:33
  568.6 23.9 %psum.91 = f32[2]{0:T(128)S(1)} all-reduce(f32[2]{0:T(128)S(1)} %get-tuple-element.20), channel_id=1, replica_groups=mesh['terms'=8] {'terms'}, use_global_device_ids=true, to_apply=%region_20.0 | all-reduce | flops 2 | bytes 16 | tf_op jit(solution)/shard_map/psum | solution.py:35
  621.4 19.8 %convert_bitcast_fusion.2 = bf16[16,2,128,16,128]{4,3,2,1,0:T(8,128)(2,1)} fusion(bf16[16,2,128,16,128]{4,2,0,3,1:T(8,128)(2,1)} %convert_bitcast_fusion.3, bf16[16,16,16]{2,1,0:T(8,128)(2,1)S(1)} %copy-done.1), kind=kOutput, calls=%fused_computation.26 | convolution fusion | flops 276824064 | bytes 33562624 | tf_op jit(solution)/shard_map/kqu,krcub->krcqb/dot_general | solution.py:30
  660.5 32.7 %reduce-scatter.15.cloned.1.call-done = f32[2,16,16,128]{3,2,0,1:T(8,128)} async-done(((f32[2,128,16,128]{3,2,0,1:T(8,128)}), f32[2,16,16,128]{3,2,0,1:T(8,128)}) %reduce-scatter.15.cloned.1.call-update) | async-done | bytes 262160 | tf_op jit(solution)/shard_map/reduce_scatter | solution.py:32
  694.3 22.2 %psum.92 = f32[2]{0:T(128)S(1)} all-reduce(f32[2]{0:T(128)S(1)} %multiply_reduce_fusion.4), channel_id=1, replica_groups=mesh['terms'=8] {'terms'}, use_global_device_ids=true, to_apply=%region_23.0 | all-reduce | flops 2 | bytes 16 | tf_op jit(solution)/shard_map/psum | solution.py:33
  717.8 23.9 %psum.93 = f32[2]{0:T(128)S(1)} all-reduce(f32[2]{0:T(128)S(1)} %get-tuple-element.16), channel_id=1, replica_groups=mesh['terms'=8] {'terms'}, use_global_device_ids=true, to_apply=%region_25.0 | all-reduce | flops 2 | bytes 16 | tf_op jit(solution)/shard_map/psum | solution.py:35
  770.6 19.8 %convert_bitcast_fusion = bf16[16,2,128,16,128]{4,3,2,1,0:T(8,128)(2,1)} fusion(bf16[16,2,128,16,128]{4,2,0,3,1:T(8,128)(2,1)} %convert_bitcast_fusion.1, bf16[16,16,16]{2,1,0:T(8,128)(2,1)S(1)} %copy-done.1), kind=kOutput, calls=%fused_computation.24 | convolution fusion | flops 276824064 | bytes 33562624 | tf_op jit(solution)/shard_map/kqu,krcub->krcqb/dot_general | solution.py:30
  814.9 27.5 %reduce-scatter.17.cloned.1.call-done = f32[2,16,16,128]{3,2,0,1:T(8,128)} async-done(((f32[2,128,16,128]{3,2,0,1:T(8,128)}), f32[2,16,16,128]{3,2,0,1:T(8,128)}) %reduce-scatter.17.cloned.1.call-update) | async-done | bytes 262160 | tf_op jit(solution)/shard_map/reduce_scatter | solution.py:32
  843.7 22.2 %psum.94 = f32[2]{0:T(128)S(1)} all-reduce(f32[2]{0:T(128)S(1)} %multiply_reduce_fusion.2), channel_id=1, replica_groups=mesh['terms'=8] {'terms'}, use_global_device_ids=true, to_apply=%region_28.0 | all-reduce | flops 2 | bytes 16 | tf_op jit(solution)/shard_map/psum | solution.py:33
  867.1 23.9 %psum.95 = f32[2]{0:T(128)S(1)} all-reduce(f32[2]{0:T(128)S(1)} %get-tuple-element.12), channel_id=1, replica_groups=mesh['terms'=8] {'terms'}, use_global_device_ids=true, to_apply=%region_30.0 | all-reduce | flops 2 | bytes 16 | tf_op jit(solution)/shard_map/psum | solution.py:35
  (112 shorter events, 299.8 us)
Async XLA Ops:
  7.2 5.0 copy-start
  7.2 13.2 %copy-start.1 = (bf16[16,16,16]{2,1,0:T(8,128)(2,1)S(1)}, bf16[16,16,16]{2,1,0:T(8,128)(2,1)}, u32[]{:S(2)}) copy-start(bf16[16,16,16]{2,1,0:T(8,128)(2,1)} %param.6) | copy-start | bytes 24580
  7.2 87.8 %reduce-scatter.7.cloned.1.call-start = ((), (), s32[]{:S(2)}) async-start(), calls=%async_computation.6 | async-start | bytes 2359296 | tf_op jit(solution)/shard_map/reduce_scatter | solution.py:32
  20.3 19.9 %copy-start.2 = (bf16[16,128,128]{2,1,0:T(8,128)(2,1)S(1)}, bf16[16,128,128]{2,1,0:T(8,128)(2,1)}, u32[]{:S(2)}) copy-start(bf16[16,128,128]{2,1,0:T(8,128)(2,1)} %param.5) | copy-start | bytes 1572868
  59.4 104.5 %all-gather.6.cloned.1.call-start = ((), (), s32[]{:S(2)}) async-start(), calls=%async_computation.7 | async-start | bytes 1179648 | tf_op jit(solution)/shard_map/all_gather | solution.py:38
  145.4 100.0 %reduce-scatter.9.cloned.1.call-start = ((), (), s32[]{:S(2)}) async-start(), calls=%async_computation.8 | async-start | bytes 2359296 | tf_op jit(solution)/shard_map/reduce_scatter | solution.py:32
  212.7 100.6 %all-gather.8.cloned.1.call-start = ((), (), s32[]{:S(2)}) async-start(), calls=%async_computation.9 | async-start | bytes 1179648 | tf_op jit(solution)/shard_map/all_gather | solution.py:38
  294.9 99.7 %reduce-scatter.11.cloned.1.call-start = ((), (), s32[]{:S(2)}) async-start(), calls=%async_computation.10 | async-start | bytes 2359296 | tf_op jit(solution)/shard_map/reduce_scatter | solution.py:32
  361.9 100.6 %all-gather.10.cloned.1.call-start = ((), (), s32[]{:S(2)}) async-start(), calls=%async_computation.11 | async-start | bytes 1179648 | tf_op jit(solution)/shard_map/all_gather | solution.py:38
  444.0 100.0 %reduce-scatter.13.cloned.1.call-start = ((), (), s32[]{:S(2)}) async-start(), calls=%async_computation.12 | async-start | bytes 2359296 | tf_op jit(solution)/shard_map/reduce_scatter | solution.py:32
  511.3 100.6 %all-gather.12.cloned.1.call-start = ((), (), s32[]{:S(2)}) async-start(), calls=%async_computation.13 | async-start | bytes 1179648 | tf_op jit(solution)/shard_map/all_gather | solution.py:38
  593.4 99.7 %reduce-scatter.15.cloned.1.call-start = ((), (), s32[]{:S(2)}) async-start(), calls=%async_computation.14 | async-start | bytes 2359296 | tf_op jit(solution)/shard_map/reduce_scatter | solution.py:32
  660.4 100.6 %all-gather.14.cloned.1.call-start = ((), (), s32[]{:S(2)}) async-start(), calls=%async_computation.15 | async-start | bytes 1179648 | tf_op jit(solution)/shard_map/all_gather | solution.py:38
  742.5 99.8 %reduce-scatter.17.cloned.1.call-start = ((), (), s32[]{:S(2)}) async-start(), calls=%async_computation.16 | async-start | bytes 2359296 | tf_op jit(solution)/shard_map/reduce_scatter | solution.py:32
Sparse Core Ops, SparseCore 0:
  59.6 35.4 reduce-scatter.6
  145.5 18.3 all-gather.5
  212.9 32.5 reduce-scatter.8
  295.0 18.3 all-gather.7
  362.0 32.5 reduce-scatter.10
  444.1 18.3 all-gather.9
  511.4 32.5 reduce-scatter.12
  593.5 18.3 all-gather.11
  660.5 32.5 reduce-scatter.14
  742.7 18.3 all-gather.13
  809.8 32.5 reduce-scatter.16
where the time goes:
time: 914 us; the launch traced here: 904 us
  waiting for transfers between devices  286 us (31%)
  blocking collectives  277 us (30%)
  matrix products  272 us (30%)
  local copies, waits for them, and re-layouts  35.3 us (4%)
  other arithmetic  18.9 us (2%)
  between operations  14.5 us (2%)
    reduce_scatter x6, waiting for transfers between devices, device_fn(): lax.psum_scatter(part_sigma, 'terms', scatter_dimension=1, tiled=True)  194 us
    psum x6, blocking collectives, device_fn(): lax.psum(jnp.sum(residual * residual, axis=(1, 2, 3)), 'terms') / n_elems  144 us
    psum x6, blocking collectives, device_fn(): alpha = lax.psum(jnp.sum(sigma * v_cur, axis=(1, 2, 3)), 'terms') / n_elems  133 us
    dot_general x6, matrix products, device_fn(): jnp.einsum('kqu,krcub->krcqb', phys_loc, right_part, preferred_element_ty...  119 us
    dot_general x6, matrix products, device_fn(): jnp.einsum('kac,krcqb->raqb', left_loc, mid_part, preferred_element_type=...  96.8 us
    all_gather x5, waiting for transfers between devices, device_fn(): lax.all_gather(v_next.astype(jnp.bfloat16), 'terms', axis=1, tiled=True)  92.3 us
    dot_general x6, matrix products, device_fn(): jnp.einsum('rcup,kbp->krcub', v_in, right_loc, preferred_element_type=jnp...  55.8 us
    transpose x6, local copies, waits for them, and re-layouts, device_fn(): jnp.einsum('kac,krcqb->raqb', left_loc, mid_part, preferred_element_type=...  18.6 us
  transfers between devices with their start and end apart: 11, of which 11 were waited for; matrix products, arithmetic and copies ran while one was open for 1% of the time, Pallas kernels for 0%

commit v1 on v0

v1 whole, which is shorter than its diff:
```python
import functools

import jax
import jax.numpy as jnp
from jax import lax
from jax.experimental import pallas as pl
from jax.experimental.pallas import tpu as pltpu
from jax.sharding import PartitionSpec as P

STEPS = 6
DEVS = 8
TERMS = 16
PAIRS = 16
BOND = 128
ROWS = 16
N_ELEMS = float(BOND * PAIRS * BOND)
MESH = pl.DeviceIdType.MESH
F32 = jnp.float32
BF16 = jnp.bfloat16


def flip(dev, bits):
    out = dev
    if bits & 1:
        out = out + 1 - 2 * lax.rem(dev, 2)
    if bits & 2:
        out = out + 2 - 4 * lax.rem(dev // 2, 2)
    if bits & 4:
        out = out + 4 - 8 * lax.rem(dev // 4, 2)
    return out


def total(x):
    return jnp.sum(jnp.sum(x, axis=0, keepdims=True), axis=1, keepdims=True)


def kernel(
    v0_ref, vfull_ref, left_ref, right_ref, phys_ref, out_ref, alpha_ref, beta_ref,
    left, right, phys, wide, v_in, y_buf, z_buf, acc, sig, v_cur, v_prev, beta_old, stats, mine, turned, got,
    r_send, r_recv, w_send, w_recv, l_send, l_recv, s_send, s_recv, g_send, g_recv, o_send, o_recv,
):
    me = lax.axis_index("terms")
    peers = {e: flip(me, e) for e in range(1, DEVS)}

    barrier = pltpu.get_barrier_semaphore()
    for e in range(1, DEVS):
        pl.semaphore_signal(barrier, inc=1, device_id=(peers[e],), device_id_type=MESH)
    pl.semaphore_wait(barrier, DEVS - 1)

    def copy(src, dst, send, recv, e):
        return pltpu.make_async_remote_copy(
            src_ref=src, dst_ref=dst, send_sem=send, recv_sem=recv, device_id=(peers[e],), device_id_type=MESH
        )

    def r_copy(e):
        rows = pl.ds(pl.multiple_of(peers[e] * ROWS, ROWS), ROWS)
        return copy(right_ref.at[:, rows, :], right.at[e], r_send.at[e], r_recv.at[e], e)

    def w_copy(e):
        return copy(phys_ref, phys.at[e], w_send.at[e], w_recv.at[e], e)

    def l_copy(e):
        return copy(left_ref, left.at[e], l_send.at[e], l_recv.at[e], e)

    def l_pass(e):
        return copy(left.at[e], left.at[e + 1], l_send.at[e + 1], l_recv.at[e + 1], 1)

    def s_copy(r, e):
        return copy(mine.at[r], stats.at[r, me], s_send.at[r, e], s_recv.at[r, e], e)

    def g_copy(r, e):
        return copy(v_in.at[r, me], v_in.at[r, me], g_send.at[r, e], g_recv.at[r, e], e)

    def g_pass(r, e):
        slot = v_in.at[r, peers[e]]
        return copy(slot, slot, g_send.at[r, e + 1], g_recv.at[r, e + 1], 1)

    def o_copy(r, e):
        rows = pl.ds(pl.multiple_of(peers[e] * ROWS, ROWS), ROWS)
        return copy(turned.at[r, :, rows, :], got.at[r, me], o_send.at[r, e], o_recv.at[r, e], e)

    for e in range(1, DEVS):
        r_copy(e).start()
        w_copy(e).start()
    for e in (1, 2, 4, 6):
        l_copy(e).start()
    own = pl.ds(pl.multiple_of(me * ROWS, ROWS), ROWS)
    right[0] = right_ref[:, own, :]
    phys[0] = phys_ref[...]
    left[0] = left_ref[...]
    v_in[...] = vfull_ref[...]
    v_cur[...] = v0_ref[...]
    v_prev[...] = jnp.zeros_like(v_prev)
    beta_old[...] = jnp.zeros_like(beta_old)
    for e in range(1, DEVS):
        r_copy(e).wait()
        w_copy(e).wait()

    sub = lax.broadcasted_iota(jnp.int32, (8, BOND), 0)
    lane = lax.broadcasted_iota(jnp.int32, (8, BOND), 1)
    eye = jnp.where(lax.rem(lane, 8) == sub, 1.0, 0.0).astype(F32)
    pick_row = lax.broadcasted_iota(jnp.int32, (PAIRS * PAIRS, BOND), 0)
    pick_col = lax.broadcasted_iota(jnp.int32, (PAIRS * PAIRS, BOND), 1) // 8

    @pl.loop(0, DEVS)
    def _(d):
        w_d = phys[d]
        spread = []
        for q in range(PAIRS):
            pick = jnp.where(pick_row == pick_col + q * PAIRS, 1.0, 0.0).astype(BF16)
            spread.append(jnp.dot(w_d, pick, preferred_element_type=F32))
        for k in range(TERMS):
            for q in range(0, PAIRS, 2):
                two = [jnp.broadcast_to(spread[q + i][k : k + 1, :], (8, BOND)) * eye for i in range(2)]
                wide[d, k, q * 8 : q * 8 + 16, :] = jnp.concatenate(two, axis=0).astype(BF16)

    for e in (2, 4, 6):
        l_copy(e).wait()
        l_pass(e).start()
    l_copy(1).wait()
    for e in (2, 4, 6):
        l_pass(e).wait()

    def chunk(r, d):
        r_d = right[d].reshape(TERMS * ROWS, BOND)
        for u in range(0, PAIRS, 2):
            v_u = jnp.concatenate([v_in[r, :, u + i].reshape(BOND, BOND) for i in range(2)], axis=1)
            y = jnp.dot(r_d, v_u, preferred_element_type=F32).reshape(TERMS, 2, 8, 2 * BOND)
            y = jnp.concatenate([y[..., :BOND], y[..., BOND:]], axis=2)
            y_buf[:, :, u * 8 : u * 8 + 16, :] = y.astype(BF16)
        for k in range(TERMS):
            y_k = jnp.concatenate([y_buf[k, 0], y_buf[k, 1]], axis=1)
            z = jnp.dot(wide[d, k], y_k, preferred_element_type=F32).astype(BF16)
            for h in range(2):
                z_buf[h * BOND : (h + 1) * BOND, k * BOND : (k + 1) * BOND] = z[:, h * BOND : (h + 1) * BOND]
        part = jnp.dot(z_buf[...], left[d].reshape(TERMS * BOND, BOND), preferred_element_type=F32)

        @pl.when(d == 0)
        def _():
            acc[...] = part

        @pl.when(d > 0)
        def _():
            acc[...] += part

    def share(r):
        s, v, vp = acc[...], v_cur[r], v_prev[r]
        d_p, n_p = total(s * v), total(v * v)
        guess = jnp.where(n_p > 0.0, d_p / jnp.where(n_p > 0.0, n_p, 1.0), 0.0)
        s = s - guess * v - beta_old[r, 0:1, :] * vp
        sig[r] = s
        rows = [d_p, n_p, guess, total(s * s), total(s * v)]
        tile = jnp.zeros((8, BOND), F32)
        for i, row in enumerate(rows):
            tile = jnp.where(sub == i, row, tile)
        mine[r] = tile
        stats[r, me] = tile
        for e in range(1, DEVS):
            s_copy(r, e).start()

    def advance(r, j, last):
        for e in range(1, DEVS):
            s_copy(r, e).wait()
        alpha = jnp.zeros((1, BOND), F32)
        for p in range(DEVS):
            alpha = alpha + stats[r, p, 0:1, :]
        alpha = alpha / N_ELEMS
        square = jnp.zeros((1, BOND), F32)
        for p in range(DEVS):
            d_p = alpha - stats[r, p, 2:3, :]
            square = square + (stats[r, p, 3:4, :] - 2.0 * d_p * stats[r, p, 4:5, :] + d_p * d_p * stats[r, p, 1:2, :])
        beta = jnp.sqrt(jnp.maximum(square, 0.0) / N_ELEMS)
        shift = alpha - mine[r, 2:3, :]
        v = v_cur[r]
        nxt = (sig[r] - shift * v) / beta
        v_prev[r] = v
        v_cur[r] = nxt
        beta_old[r] = jnp.broadcast_to(beta, (8, BOND))
        alpha_ref[r, j] = jnp.broadcast_to(alpha, (8, BOND))
        beta_ref[r, j] = jnp.broadcast_to(beta, (8, BOND))
        halves = nxt.reshape(2, PAIRS, 8, BOND)
        joined = jnp.concatenate([halves[0], halves[1]], axis=1)
        if last:
            pass
        else:
            v_in[r, me] = joined.astype(BF16)
            for e in (1, 2, 4, 6):
                g_copy(r, e).start()
        for g in range(2):
            turned[r, g] = joined[g * 8 : (g + 1) * 8].reshape(BOND, BOND).T
        for e in range(1, DEVS):
            o_copy(r, e).start()
        got[r, me] = turned[r, :, own, :]

    def relay(r):
        for e in (2, 4, 6):
            g_copy(r, e).wait()
            g_pass(r, e).start()

    def arrive(r):
        g_copy(r, 1).wait()
        for e in (2, 4, 6):
            g_pass(r, e).wait()

    def collect(r, j):
        for e in range(1, DEVS):
            o_copy(r, e).wait()
        chunk_of = lax.broadcasted_iota(jnp.int32, (ROWS, BOND), 1) // 16
        for g in range(2):
            x = [got[r, p, g] for p in range(DEVS)]
            for bit in (1, 2, 4):
                odd = lax.rem(chunk_of // bit, 2) == 1
                for p in range(DEVS):
                    if p & bit:
                        continue
                    low, high = x[p], x[p + bit]
                    x[p] = jnp.where(odd, pltpu.roll(high, 16 * bit, 1), low)
                    x[p + bit] = jnp.where(odd, high, pltpu.roll(low, BOND - 16 * bit, 1))
            for q in range(8):
                out_ref[r, j, g * 8 + q] = x[q]

    @pl.loop(0, 2 * STEPS)
    def _(t):
        r, j = lax.rem(t, 2), t // 2
        pr, pj = 1 - r, (t - 1) // 2

        @pl.when(t >= 2)
        def _():
            arrive(r)

        @pl.loop(0, DEVS)
        def _(d):
            chunk(r, d)

            @pl.when(jnp.logical_and(d == 0, jnp.logical_and(t >= 1, t < 2 * STEPS - 1)))
            def _():
                advance(pr, pj, False)

            @pl.when(jnp.logical_and(d == 0, t == 2 * STEPS - 1))
            def _():
                advance(pr, pj, True)

            @pl.when(jnp.logical_and(d == 3, t >= 2))
            def _():
                collect(r, j - 1)

            @pl.when(jnp.logical_and(d == 5, jnp.logical_and(t >= 1, t < 2 * STEPS - 1)))
            def _():
                relay(pr)

        share(r)

    advance(1, STEPS - 1, True)
    collect(0, STEPS - 1)
    collect(1, STEPS - 1)


def solution(mesh):
    def device_fn(psi, left_loc, phys_loc, right_loc):
        roots = psi.shape[0]
        me = lax.axis_index("terms")
        psi_mat = psi.reshape(roots, BOND, PAIRS, BOND)
        norms = jnp.sqrt(jnp.sum(psi_mat * psi_mat, axis=(1, 2, 3)) / N_ELEMS)
        v_full = psi_mat / norms[:, None, None, None]
        first = lax.dynamic_slice_in_dim(v_full, me * ROWS, ROWS, axis=1)
        across = jnp.transpose(v_full, (0, 2, 3, 1))
        v_bf = across.astype(BF16).reshape(roots, PAIRS, DEVS, ROWS, BOND).transpose(0, 2, 1, 3, 4)
        v_own = lax.dynamic_slice_in_dim(across, me * ROWS, ROWS, axis=2)
        v_own = v_own.reshape(roots, PAIRS, 2, 8, BOND).transpose(0, 2, 1, 3, 4).reshape(roots, 2 * BOND, BOND)
        vm = pl.BlockSpec(memory_space=pltpu.VMEM)
        dma = pltpu.SemaphoreType.DMA
        rest, alpha, beta = pl.pallas_call(
            kernel,
            out_shape=(
                jax.ShapeDtypeStruct((roots, STEPS, PAIRS, ROWS, BOND), F32),
                jax.ShapeDtypeStruct((roots, STEPS, 8, BOND), F32),
                jax.ShapeDtypeStruct((roots, STEPS, 8, BOND), F32),
            ),
            in_specs=[vm] * 5,
            out_specs=(vm, vm, vm),
            scratch_shapes=[
                pltpu.VMEM((DEVS, TERMS, BOND, BOND), BF16),
                pltpu.VMEM((DEVS, TERMS, ROWS, BOND), BF16),
                pltpu.VMEM((DEVS, TERMS, PAIRS * PAIRS), BF16),
                pltpu.VMEM((DEVS, TERMS, BOND, BOND), BF16),
                pltpu.VMEM((roots, DEVS, PAIRS, ROWS, BOND), BF16),
                pltpu.VMEM((TERMS, 2, BOND, BOND), BF16),
                pltpu.VMEM((2 * BOND, TERMS * BOND), BF16),
                pltpu.VMEM((2 * BOND, BOND), F32),
                pltpu.VMEM((roots, 2 * BOND, BOND), F32),
                pltpu.VMEM((roots, 2 * BOND, BOND), F32),
                pltpu.VMEM((roots, 2 * BOND, BOND), F32),
                pltpu.VMEM((roots, 8, BOND), F32),
                pltpu.VMEM((roots, DEVS, 8, BOND), F32),
                pltpu.VMEM((roots, 8, BOND), F32),
                pltpu.VMEM((roots, 2, BOND, BOND), F32),
                pltpu.VMEM((roots, DEVS, 2, ROWS, BOND), F32),
                dma((DEVS,)), dma((DEVS,)), dma((DEVS,)), dma((DEVS,)), dma((DEVS,)), dma((DEVS,)),
                dma((roots, DEVS)), dma((roots, DEVS)), dma((roots, DEVS)), dma((roots, DEVS)),
                dma((roots, DEVS)), dma((roots, DEVS)),
            ],
            compiler_params=pltpu.CompilerParams(
                collective_id=0, has_side_effects=True, vmem_limit_bytes=56 * 1024 * 1024
            ),
        )(v_own, v_bf, left_loc, right_loc, phys_loc.reshape(TERMS, PAIRS * PAIRS))
        rest = jnp.transpose(rest, (0, 1, 3, 2, 4))
        vecs = jnp.concatenate([first[:, None], rest], axis=1)
        vecs = vecs.reshape(roots, STEPS + 1, ROWS, psi.shape[2], psi.shape[3], BOND)
        return vecs, alpha[:, :, 0, 0], beta[:, :, 0, 0]

    return jax.shard_map(
        device_fn, mesh=mesh, in_specs=(P(), P("terms"), P("terms"), P("terms")),
        out_specs=(P(None, None, "terms"), P(), P()), check_vma=False,
    )
```

time: 914 us -> 205 us (0.22); the launches traced: 904 us -> 205 us
  waiting for transfers between devices: 286 us -> 0 us
  blocking collectives: 277 us -> 0 us
  matrix products: 272 us -> 0 us
  Pallas kernels: 0 us -> 186 us
  local copies, waits for them, and re-layouts: 35.3 us -> 14.5 us
  other arithmetic: 18.9 us -> 3.82 us
  between operations: 14.5 us -> 0.69 us
    psum x12 -> x0, blocking collectives: 277 us -> none  [the longest x6 144 us: device_fn(): lax.psum(jnp.sum(residual * residual, axis=(1, 2, 3)), 'terms') / n_elems]
    dot_general x18 -> x0, matrix products: 272 us -> none  [the longest x6 119 us: device_fn(): jnp.einsum('kqu,krcub->krcqb', phys_loc, right_part, preferred_element_ty...]
    reduce_scatter x6 -> x0, waiting for transfers between devices: 194 us -> none  [device_fn(): lax.psum_scatter(part_sigma, 'terms', scatter_dimension=1, tiled=True)]
    pallas_call x0 -> x1, Pallas kernels: none -> 186 us  [device_fn(): pl.pallas_call(kernel, out_shape=(jax.ShapeDtypeStruct((roots, STEPS, PAI...]
    all_gather x5 -> x0, waiting for transfers between devices: 92.3 us -> none  [device_fn(): lax.all_gather(v_next.astype(jnp.bfloat16), 'terms', axis=1, tiled=True)]
    transpose x6 -> x1, local copies, waits for them, and re-layouts: 18.6 us -> 0.73 us  [device_fn(): v_own.reshape(roots, PAIRS, 2, 8, BOND).transpose(0, 2, 1, 3, 4)]
    reduce_sum x13 -> x1, other arithmetic: 16.7 us -> 0.65 us  [device_fn(): norms = jnp.sqrt(jnp.sum(psi_mat * psi_mat, axis=(1, 2, 3)) / N_ELEMS)]
  transfers between devices with their start and end apart: 11 -> 0, of which waited for: 11 -> 0; matrix products, arithmetic and copies ran while one was open for 1% -> 0% of each run, Pallas kernels for 0% -> 0%
where the time goes in v1:
time: 205 us
  Pallas kernels  186 us (91%)
  local copies, waits for them, and re-layouts  14.5 us (7%)
  other arithmetic  3.82 us (2%)
    pallas_call x1, Pallas kernels, device_fn(): pl.pallas_call(kernel, out_shape=(jax.ShapeDtypeStruct((roots, STEPS, PAI...  186 us
    dynamic_slice x2, local copies, waits for them, and re-layouts, device_fn(): v_own = lax.dynamic_slice_in_dim(across, me * ROWS, ROWS, axis=2)  4.11 us

profile of v1, /device:TPU:0, one launch (start us, length us, event | category | flops | bytes accessed | tf_op | source)
XLA Modules:
  0.0 205.2 jit_solution(7132042823907608645)
XLA Ops:
  0.6 0.0 copy-start
  0.6 2.4 %copy.12 = f32[2,128,4,4,128]{4,1,3,2,0:T(8,128)S(1)} copy(f32[2,128,4,4,128]{4,3,2,1,0:T(4,128)} %param.4) | data formatting | bytes 4194304 | tf_op args[0]
  3.0 0.0 copy-done
  3.0 0.7 multiply_reduce_fusion
  3.7 1.5 convert_bitcast_fusion
  5.1 2.0 dynamic-slice_bitcast_fusion
  7.1 2.2 %copy.13 = f32[2,16,16,128]{3,2,1,0:T(8,128)S(1)} copy(f32[2,16,16,128]{2,3,1,0:T(8,128)} %dynamic-slice_bitcast_fusion) | data formatting | bytes 524288 | tf_op jit(solution)/shard_map/dynamic_slice | solution.py:268
  9.3 0.7 copy.14
  10.0 0.0 copy-start.1
  10.0 1.6 copy.15
  11.6 1.2 copy.20
  12.9 0.0 copy-done.1
  12.9 0.7 reshape.33.phys_ref
  13.6 186.2 %shard_map.67 = (f32[2,6,16,16,128]{4,3,2,1,0:T(8,128)}, f32[2,6,8,128]{3,2,1,0:T(8,128)}, f32[2,6,8,128]{3,2,1,0:T(8,128)}) custom-call(f32[2,256,128]{2,1,0:T(8,128)} %bitcast.21, bf16[2,8,16,16,128]{4,3,2,1,0:T(8,128)(2,1)} %bitcast.18, bf16[16,128,128]{2,1,0:T(8,128)(2,1)} %left_ref.1, bf16[16,128,128]{2,1,0:T(8,128)(2,1)} %right_ref.1, ...), custom_call_target="tpu_custom_call" | custom-call | tf_op jit(solution)/shard_map/pallas_call | solution.py:272
  199.8 1.5 slice_reduce_fusion
  201.3 2.0 copy.18
  203.4 0.1 copy.17
  203.5 1.7 pad_maximum_fusion
  (2 shorter events, 0.0 us)
Async XLA Ops:
  0.6 2.4 %copy-start = (f32[2,128,4,4,128]{4,3,2,1,0:T(4,128)S(1)}, f32[2,128,4,4,128]{4,3,2,1,0:T(4,128)}, u32[]{:S(2)}) copy-start(f32[2,128,4,4,128]{4,3,2,1,0:T(4,128)} %param.4) | copy-start | bytes 6291460
  10.0 2.9 %copy-start.1 = (bf16[16,16,16]{2,1,0:T(8,128)(2,1)S(1)}, bf16[16,16,16]{2,1,0:T(8,128)(2,1)}, u32[]{:S(2)}) copy-start(bf16[16,16,16]{2,1,0:T(8,128)(2,1)} %param.6) | copy-start | bytes 24580

commit v2 on v1

--- a/solution.py
+++ b/solution.py
@@ -232,11 +232,11 @@
         def _(d):
             chunk(r, d)
 
-            @pl.when(jnp.logical_and(d == 0, jnp.logical_and(t >= 1, t < 2 * STEPS - 1)))
+            @pl.when(jnp.logical_and(d == 2, jnp.logical_and(t >= 1, t < 2 * STEPS - 1)))
             def _():
                 advance(pr, pj, False)
 
-            @pl.when(jnp.logical_and(d == 0, t == 2 * STEPS - 1))
+            @pl.when(jnp.logical_and(d == 2, t == 2 * STEPS - 1))
             def _():
                 advance(pr, pj, True)
 
@@ -244,7 +244,7 @@
             def _():
                 collect(r, j - 1)
 
-            @pl.when(jnp.logical_and(d == 5, jnp.logical_and(t >= 1, t < 2 * STEPS - 1)))
+            @pl.when(jnp.logical_and(d == 6, jnp.logical_and(t >= 1, t < 2 * STEPS - 1)))
             def _():
                 relay(pr)
 

time: 205 us -> 192 us (0.937)
  Pallas kernels: 186 us -> 173 us
    pallas_call x1, Pallas kernels: 186 us -> 173 us  [device_fn(): pl.pallas_call(kernel, out_shape=(jax.ShapeDtypeStruct((roots, STEPS, PAI...]
where the time goes in v2:
time: 192 us
  Pallas kernels  173 us (90%)
  local copies, waits for them, and re-layouts  14.5 us (8%)
  other arithmetic  3.82 us (2%)
    pallas_call x1, Pallas kernels, device_fn(): pl.pallas_call(kernel, out_shape=(jax.ShapeDtypeStruct((roots, STEPS, PAI...  173 us
    dynamic_slice x2, local copies, waits for them, and re-layouts, device_fn(): v_own = lax.dynamic_slice_in_dim(across, me * ROWS, ROWS, axis=2)  4.11 us

profile of v2, /device:TPU:0, one launch (start us, length us, event | category | flops | bytes accessed | tf_op | source)
XLA Modules:
  0.0 192.0 jit_solution(9069049387823471591)
XLA Ops:
  0.6 0.0 copy-start
  0.6 2.4 %copy.12 = f32[2,128,4,4,128]{4,1,3,2,0:T(8,128)S(1)} copy(f32[2,128,4,4,128]{4,3,2,1,0:T(4,128)} %param.4) | data formatting | bytes 4194304 | tf_op args[0]
  3.0 0.0 copy-done
  3.0 0.7 multiply_reduce_fusion
  3.7 1.5 convert_bitcast_fusion
  5.1 2.0 %dynamic-slice_bitcast_fusion = f32[2,16,16,128]{2,3,1,0:T(8,128)} fusion(f32[2,128,16,128]{3,1,2,0:T(8,128)S(1)} %get-tuple-element.10, s32[]{:T(128)S(6)} %select_n.4), kind=kLoop, calls=%fused_computation | loop fusion | bytes 524292 | tf_op jit(solution)/shard_map/dynamic_slice | solution.py:268
  7.1 2.2 %copy.13 = f32[2,16,16,128]{3,2,1,0:T(8,128)S(1)} copy(f32[2,16,16,128]{2,3,1,0:T(8,128)} %dynamic-slice_bitcast_fusion) | data formatting | bytes 524288 | tf_op jit(solution)/shard_map/dynamic_slice | solution.py:268
  9.3 0.7 copy.14
  10.0 0.0 copy-start.1
  10.0 1.6 copy.15
  11.6 1.2 copy.20
  12.9 0.0 copy-done.1
  12.9 0.7 reshape.33.phys_ref
  13.6 173.1 %shard_map.67 = (f32[2,6,16,16,128]{4,3,2,1,0:T(8,128)}, f32[2,6,8,128]{3,2,1,0:T(8,128)}, f32[2,6,8,128]{3,2,1,0:T(8,128)}) custom-call(f32[2,256,128]{2,1,0:T(8,128)} %bitcast.21, bf16[2,8,16,16,128]{4,3,2,1,0:T(8,128)(2,1)} %bitcast.18, bf16[16,128,128]{2,1,0:T(8,128)(2,1)} %left_ref.1, bf16[16,128,128]{2,1,0:T(8,128)(2,1)} %right_ref.1, ...), custom_call_target="tpu_custom_call" | custom-call | tf_op jit(solution)/shard_map/pallas_call | solution.py:272
  186.7 1.5 slice_reduce_fusion
  188.2 2.0 %copy.18 = f32[2,6,16,4,4,128]{5,4,3,2,1,0:T(4,128)S(1)} copy(f32[2,6,16,4,4,128]{5,2,4,3,1,0:T(8,128)} %bitcast.20) | data formatting | bytes 3145728 | tf_op jit(solution)/shard_map/concatenate | solution.py:307
  190.2 0.1 copy.17
  190.3 1.7 pad_maximum_fusion
  (2 shorter events, 0.0 us)
Async XLA Ops:
  0.6 2.4 %copy-start = (f32[2,128,4,4,128]{4,3,2,1,0:T(4,128)S(1)}, f32[2,128,4,4,128]{4,3,2,1,0:T(4,128)}, u32[]{:S(2)}) copy-start(f32[2,128,4,4,128]{4,3,2,1,0:T(4,128)} %param.4) | copy-start | bytes 6291460
  10.0 2.9 %copy-start.1 = (bf16[16,16,16]{2,1,0:T(8,128)(2,1)S(1)}, bf16[16,16,16]{2,1,0:T(8,128)(2,1)}, u32[]{:S(2)}) copy-start(bf16[16,16,16]{2,1,0:T(8,128)(2,1)} %param.6) | copy-start | bytes 24580

commit v3 on v2

--- a/solution.py
+++ b/solution.py
@@ -14,6 +14,8 @@
 BOND = 128
 ROWS = 16
 N_ELEMS = float(BOND * PAIRS * BOND)
+FORM_AFTER = 2
+RELAY_AFTER = 6
 MESH = pl.DeviceIdType.MESH
 F32 = jnp.float32
 BF16 = jnp.bfloat16
@@ -35,8 +37,9 @@
 
 
 def kernel(
-    v0_ref, vfull_ref, left_ref, right_ref, phys_ref, out_ref, alpha_ref, beta_ref,
-    left, right, phys, wide, v_in, y_buf, z_buf, acc, sig, v_cur, v_prev, beta_old, stats, mine, turned, got,
+    psi_ref, left_ref, right_ref, phys_ref, out_ref, alpha_ref, beta_ref,
+    left, right, phys, wide, v_in, y_buf0, y_buf1, z_buf0, z_buf1, acc, sig, v_cur, v_prev, beta_old, stats, mine,
+    turned, got, across, numbers,
     r_send, r_recv, w_send, w_recv, l_send, l_recv, s_send, s_recv, g_send, g_recv, o_send, o_recv,
 ):
     me = lax.axis_index("terms")
@@ -88,10 +91,33 @@
     right[0] = right_ref[:, own, :]
     phys[0] = phys_ref[...]
     left[0] = left_ref[...]
-    v_in[...] = vfull_ref[...]
-    v_cur[...] = v0_ref[...]
     v_prev[...] = jnp.zeros_like(v_prev)
     beta_old[...] = jnp.zeros_like(beta_old)
+    numbers[...] = jnp.zeros_like(numbers)
+
+    @pl.loop(0, 2)
+    def _(r):
+        acc[0:BOND, :] = jnp.zeros((BOND, BOND), F32)
+
+        @pl.loop(0, 4)
+        def _(s):
+            for t in range(4):
+                x = psi_ref[r, :, s, t, :]
+                acc[0:BOND, :] += x * x
+                across[s * 4 + t] = x.T
+
+        norm = jnp.sqrt(total(acc[0:BOND, :]) / N_ELEMS)
+
+        @pl.loop(0, PAIRS)
+        def _(u):
+            v_in[r, :, u] = (across[u] / norm).astype(BF16).reshape(DEVS, ROWS, BOND)
+            two = across[u, own, :] / norm
+            row = pl.multiple_of(u * 8, 8)
+            v_cur[r, pl.ds(row, 8), :] = two[0:8]
+            v_cur[r, pl.ds(row + BOND, 8), :] = two[8:16]
+
+        out_ref[r, 0] = psi_ref[r, own] / norm.reshape(1, 1, 1, 1)
+
     for e in range(1, DEVS):
         r_copy(e).wait()
         w_copy(e).wait()
@@ -122,6 +148,7 @@
         l_pass(e).wait()
 
     def chunk(r, d):
+        y_buf, z_buf = ((y_buf0, z_buf0), (y_buf1, z_buf1))[d % 2]
         r_d = right[d].reshape(TERMS * ROWS, BOND)
         for u in range(0, PAIRS, 2):
             v_u = jnp.concatenate([v_in[r, :, u + i].reshape(BOND, BOND) for i in range(2)], axis=1)
@@ -134,13 +161,9 @@
             for h in range(2):
                 z_buf[h * BOND : (h + 1) * BOND, k * BOND : (k + 1) * BOND] = z[:, h * BOND : (h + 1) * BOND]
         part = jnp.dot(z_buf[...], left[d].reshape(TERMS * BOND, BOND), preferred_element_type=F32)
-
-        @pl.when(d == 0)
-        def _():
+        if d == 0:
             acc[...] = part
-
-        @pl.when(d > 0)
-        def _():
+        else:
             acc[...] += part
 
     def share(r):
@@ -176,8 +199,9 @@
         v_prev[r] = v
         v_cur[r] = nxt
         beta_old[r] = jnp.broadcast_to(beta, (8, BOND))
-        alpha_ref[r, j] = jnp.broadcast_to(alpha, (8, BOND))
-        beta_ref[r, j] = jnp.broadcast_to(beta, (8, BOND))
+        here = jnp.logical_and(sub == r, lane == j)
+        numbers[0] = jnp.where(here, alpha, numbers[0])
+        numbers[1] = jnp.where(here, beta, numbers[1])
         halves = nxt.reshape(2, PAIRS, 8, BOND)
         joined = jnp.concatenate([halves[0], halves[1]], axis=1)
         if last:
@@ -217,7 +241,8 @@
                     x[p] = jnp.where(odd, pltpu.roll(high, 16 * bit, 1), low)
                     x[p + bit] = jnp.where(odd, high, pltpu.roll(low, BOND - 16 * bit, 1))
             for q in range(8):
-                out_ref[r, j, g * 8 + q] = x[q]
+                pair = g * 8 + q
+                out_ref[r, j + 1, :, pair // 4, pair % 4, :] = x[q]
 
     @pl.loop(0, 2 * STEPS)
     def _(t):
@@ -228,55 +253,50 @@
         def _():
             arrive(r)
 
-        @pl.loop(0, DEVS)
-        def _(d):
+        for d in range(DEVS):
             chunk(r, d)
-
-            @pl.when(jnp.logical_and(d == 2, jnp.logical_and(t >= 1, t < 2 * STEPS - 1)))
-            def _():
-                advance(pr, pj, False)
-
-            @pl.when(jnp.logical_and(d == 2, t == 2 * STEPS - 1))
-            def _():
-                advance(pr, pj, True)
-
-            @pl.when(jnp.logical_and(d == 3, t >= 2))
-            def _():
-                collect(r, j - 1)
-
-            @pl.when(jnp.logical_and(d == 6, jnp.logical_and(t >= 1, t < 2 * STEPS - 1)))
-            def _():
-                relay(pr)
+            if d == FORM_AFTER:
+
+                @pl.when(jnp.logical_and(t >= 1, t < 2 * STEPS - 1))
+                def _():
+                    advance(pr, pj, False)
+
+                @pl.when(t == 2 * STEPS - 1)
+                def _():
+                    advance(pr, pj, True)
+
+                @pl.when(t >= 2)
+                def _():
+                    collect(r, j - 1)
+
+            if d == RELAY_AFTER:
+
+                @pl.when(jnp.logical_and(t >= 1, t < 2 * STEPS - 1))
+                def _():
+                    relay(pr)
 
         share(r)
 
     advance(1, STEPS - 1, True)
     collect(0, STEPS - 1)
     collect(1, STEPS - 1)
+    alpha_ref[...] = numbers[0, 0:2, 0:STEPS]
+    beta_ref[...] = numbers[1, 0:2, 0:STEPS]
 
 
 def solution(mesh):
     def device_fn(psi, left_loc, phys_loc, right_loc):
         roots = psi.shape[0]
-        me = lax.axis_index("terms")
-        psi_mat = psi.reshape(roots, BOND, PAIRS, BOND)
-        norms = jnp.sqrt(jnp.sum(psi_mat * psi_mat, axis=(1, 2, 3)) / N_ELEMS)
-        v_full = psi_mat / norms[:, None, None, None]
-        first = lax.dynamic_slice_in_dim(v_full, me * ROWS, ROWS, axis=1)
-        across = jnp.transpose(v_full, (0, 2, 3, 1))
-        v_bf = across.astype(BF16).reshape(roots, PAIRS, DEVS, ROWS, BOND).transpose(0, 2, 1, 3, 4)
-        v_own = lax.dynamic_slice_in_dim(across, me * ROWS, ROWS, axis=2)
-        v_own = v_own.reshape(roots, PAIRS, 2, 8, BOND).transpose(0, 2, 1, 3, 4).reshape(roots, 2 * BOND, BOND)
         vm = pl.BlockSpec(memory_space=pltpu.VMEM)
         dma = pltpu.SemaphoreType.DMA
-        rest, alpha, beta = pl.pallas_call(
+        return pl.pallas_call(
             kernel,
             out_shape=(
-                jax.ShapeDtypeStruct((roots, STEPS, PAIRS, ROWS, BOND), F32),
-                jax.ShapeDtypeStruct((roots, STEPS, 8, BOND), F32),
-                jax.ShapeDtypeStruct((roots, STEPS, 8, BOND), F32),
+                jax.ShapeDtypeStruct((roots, STEPS + 1, ROWS) + psi.shape[2:], F32),
+                jax.ShapeDtypeStruct((roots, STEPS), F32),
+                jax.ShapeDtypeStruct((roots, STEPS), F32),
             ),
-            in_specs=[vm] * 5,
+            in_specs=[vm] * 4,
             out_specs=(vm, vm, vm),
             scratch_shapes=[
                 pltpu.VMEM((DEVS, TERMS, BOND, BOND), BF16),
@@ -285,6 +305,8 @@
                 pltpu.VMEM((DEVS, TERMS, BOND, BOND), BF16),
                 pltpu.VMEM((roots, DEVS, PAIRS, ROWS, BOND), BF16),
                 pltpu.VMEM((TERMS, 2, BOND, BOND), BF16),
+                pltpu.VMEM((TERMS, 2, BOND, BOND), BF16),
+                pltpu.VMEM((2 * BOND, TERMS * BOND), BF16),
                 pltpu.VMEM((2 * BOND, TERMS * BOND), BF16),
                 pltpu.VMEM((2 * BOND, BOND), F32),
                 pltpu.VMEM((roots, 2 * BOND, BOND), F32),
@@ -295,6 +317,8 @@
                 pltpu.VMEM((roots, 8, BOND), F32),
                 pltpu.VMEM((roots, 2, BOND, BOND), F32),
                 pltpu.VMEM((roots, DEVS, 2, ROWS, BOND), F32),
+                pltpu.VMEM((PAIRS, BOND, BOND), F32),
+                pltpu.VMEM((2, 8, BOND), F32),
                 dma((DEVS,)), dma((DEVS,)), dma((DEVS,)), dma((DEVS,)), dma((DEVS,)), dma((DEVS,)),
                 dma((roots, DEVS)), dma((roots, DEVS)), dma((roots, DEVS)), dma((roots, DEVS)),
                 dma((roots, DEVS)), dma((roots, DEVS)),
@@ -302,11 +326,7 @@
             compiler_params=pltpu.CompilerParams(
                 collective_id=0, has_side_effects=True, vmem_limit_bytes=56 * 1024 * 1024
             ),
-        )(v_own, v_bf, left_loc, right_loc, phys_loc.reshape(TERMS, PAIRS * PAIRS))
-        rest = jnp.transpose(rest, (0, 1, 3, 2, 4))
-        vecs = jnp.concatenate([first[:, None], rest], axis=1)
-        vecs = vecs.reshape(roots, STEPS + 1, ROWS, psi.shape[2], psi.shape[3], BOND)
-        return vecs, alpha[:, :, 0, 0], beta[:, :, 0, 0]
+        )(psi, left_loc, right_loc, phys_loc.reshape(TERMS, PAIRS * PAIRS))
 
     return jax.shard_map(
         device_fn, mesh=mesh, in_specs=(P(), P("terms"), P("terms"), P("terms")),

time: 192 us -> 175 us (0.911)
  local copies, waits for them, and re-layouts: 14.5 us -> 5.79 us
  Pallas kernels: 173 us -> 168 us
  other arithmetic: 3.82 us -> 0 us
    pallas_call x1, Pallas kernels: 173 us -> 168 us  [device_fn(): pl.pallas_call(kernel, out_shape=(jax.ShapeDtypeStruct((roots, STEPS + 1,...]
    dynamic_slice x3 -> x0, local copies, waits for them, and re-layouts: 4.14 us -> none  [the longest x2 4.11 us: device_fn(): v_own = lax.dynamic_slice_in_dim(across, me * ROWS, ROWS, axis=2)]
    concatenate x2 -> x0, local copies, waits for them, and re-layouts: 2.12 us -> none  [device_fn(): vecs = jnp.concatenate([first[:, None], rest], axis=1)]
    unnamed x5 -> x7, local copies, waits for them, and re-layouts: 2.37 us -> 4.23 us
where the time goes in v3:
time: 175 us
  Pallas kernels  168 us (96%)
  local copies, waits for them, and re-layouts  5.79 us (3%)
    pallas_call x1, Pallas kernels, device_fn(): pl.pallas_call(kernel, out_shape=(jax.ShapeDtypeStruct((roots, STEPS + 1,...  168 us
    unnamed x7, local copies, waits for them, and re-layouts  4.23 us

profile of v3, /device:TPU:0, one launch (start us, length us, event | category | flops | bytes accessed | tf_op | source)
XLA Modules:
  0.0 174.7 jit_solution(3992659977978349640)
XLA Ops:
  0.6 1.6 reshape.9.phys_ref
  2.2 168.2 %shard_map.67 = (f32[2,7,16,4,4,128]{5,4,3,2,1,0:T(4,128)}, f32[2,6]{1,0:T(2,128)}, f32[2,6]{1,0:T(2,128)}) custom-call(f32[2,128,4,4,128]{4,3,2,1,0:T(4,128)} %psi_ref.1, bf16[16,128,128]{2,1,0:T(8,128)(2,1)} %left_ref.1, bf16[16,128,128]{2,1,0:T(8,128)(2,1)} %right_ref.1, bf16[16,256]{1,0:T(8,128)(2,1)} %reshape.9.phys_ref), custom_call_target="tpu_custom_call" | custom-call | tf_op jit(solution)/shard_map/pallas_call | solution.py:292
  170.4 0.0 copy-start.1
  170.5 0.0 copy-start
  170.5 3.1 %copy.10 = f32[2,7,16,4,4,128]{5,4,3,2,1,0:T(4,128)} copy(f32[2,7,16,4,4,128]{5,4,3,2,1,0:T(4,128)} %get-tuple-element.6) | data formatting | bytes 3670016
  173.6 0.0 copy-done.1
  173.6 0.6 copy.11
  174.1 0.0 copy-done
  174.1 0.6 copy.12
Async XLA Ops:
  170.4 3.1 %copy-start.1 = (f32[2,6]{1,0:T(2,128)S(1)}, f32[2,6]{1,0:T(2,128)}, u32[]{:S(2)}) copy-start(f32[2,6]{1,0:T(2,128)} %get-tuple-element.7) | copy-start | bytes 148
  170.5 3.7 %copy-start = (f32[2,6]{1,0:T(2,128)S(1)}, f32[2,6]{1,0:T(2,128)}, u32[]{:S(2)}) copy-start(f32[2,6]{1,0:T(2,128)} %get-tuple-element.8) | copy-start | bytes 148

commit v4 on v3

--- a/solution.py
+++ b/solution.py
@@ -14,8 +14,8 @@
 BOND = 128
 ROWS = 16
 N_ELEMS = float(BOND * PAIRS * BOND)
-FORM_AFTER = 2
-RELAY_AFTER = 6
+FORM_AFTER = 1
+COLLECT_AFTER = 5
 MESH = pl.DeviceIdType.MESH
 F32 = jnp.float32
 BF16 = jnp.bfloat16
@@ -82,11 +82,11 @@
         rows = pl.ds(pl.multiple_of(peers[e] * ROWS, ROWS), ROWS)
         return copy(turned.at[r, :, rows, :], got.at[r, me], o_send.at[r, e], o_recv.at[r, e], e)
 
-    for e in range(1, DEVS):
-        r_copy(e).start()
-        w_copy(e).start()
-    for e in (1, 2, 4, 6):
-        l_copy(e).start()
+    for both in ((1,), (2, 3), (4, 5), (6, 7)):
+        for e in both:
+            r_copy(e).start()
+            w_copy(e).start()
+        l_copy(2 * (both[0] // 2) if both[0] > 1 else 1).start()
     own = pl.ds(pl.multiple_of(me * ROWS, ROWS), ROWS)
     right[0] = right_ref[:, own, :]
     phys[0] = phys_ref[...]
@@ -118,18 +118,13 @@
 
         out_ref[r, 0] = psi_ref[r, own] / norm.reshape(1, 1, 1, 1)
 
-    for e in range(1, DEVS):
-        r_copy(e).wait()
-        w_copy(e).wait()
-
     sub = lax.broadcasted_iota(jnp.int32, (8, BOND), 0)
     lane = lax.broadcasted_iota(jnp.int32, (8, BOND), 1)
     eye = jnp.where(lax.rem(lane, 8) == sub, 1.0, 0.0).astype(F32)
     pick_row = lax.broadcasted_iota(jnp.int32, (PAIRS * PAIRS, BOND), 0)
     pick_col = lax.broadcasted_iota(jnp.int32, (PAIRS * PAIRS, BOND), 1) // 8
 
-    @pl.loop(0, DEVS)
-    def _(d):
+    def widen(d):
         w_d = phys[d]
         spread = []
         for q in range(PAIRS):
@@ -140,15 +135,7 @@
                 two = [jnp.broadcast_to(spread[q + i][k : k + 1, :], (8, BOND)) * eye for i in range(2)]
                 wide[d, k, q * 8 : q * 8 + 16, :] = jnp.concatenate(two, axis=0).astype(BF16)
 
-    for e in (2, 4, 6):
-        l_copy(e).wait()
-        l_pass(e).start()
-    l_copy(1).wait()
-    for e in (2, 4, 6):
-        l_pass(e).wait()
-
-    def chunk(r, d):
-        y_buf, z_buf = ((y_buf0, z_buf0), (y_buf1, z_buf1))[d % 2]
+    def chunk(r, d, y_buf, z_buf, first):
         r_d = right[d].reshape(TERMS * ROWS, BOND)
         for u in range(0, PAIRS, 2):
             v_u = jnp.concatenate([v_in[r, :, u + i].reshape(BOND, BOND) for i in range(2)], axis=1)
@@ -161,7 +148,7 @@
             for h in range(2):
                 z_buf[h * BOND : (h + 1) * BOND, k * BOND : (k + 1) * BOND] = z[:, h * BOND : (h + 1) * BOND]
         part = jnp.dot(z_buf[...], left[d].reshape(TERMS * BOND, BOND), preferred_element_type=F32)
-        if d == 0:
+        if first:
             acc[...] = part
         else:
             acc[...] += part
@@ -178,7 +165,7 @@
             tile = jnp.where(sub == i, row, tile)
         mine[r] = tile
         stats[r, me] = tile
-        for e in range(1, DEVS):
+        for e in (6, 7, 2, 3, 4, 5, 1):
             s_copy(r, e).start()
 
     def advance(r, j, last):
@@ -208,16 +195,18 @@
             pass
         else:
             v_in[r, me] = joined.astype(BF16)
-            for e in (1, 2, 4, 6):
+            for e in (6, 2, 4, 1):
                 g_copy(r, e).start()
         for g in range(2):
             turned[r, g] = joined[g * 8 : (g + 1) * 8].reshape(BOND, BOND).T
-        for e in range(1, DEVS):
+
+    def post(r):
+        for e in (6, 7, 2, 3, 4, 5, 1):
             o_copy(r, e).start()
         got[r, me] = turned[r, :, own, :]
 
     def relay(r):
-        for e in (2, 4, 6):
+        for e in (4, 6, 2):
             g_copy(r, e).wait()
             g_pass(r, e).start()
 
@@ -244,7 +233,34 @@
                 pair = g * 8 + q
                 out_ref[r, j + 1, :, pair // 4, pair % 4, :] = x[q]
 
-    @pl.loop(0, 2 * STEPS)
+    acc[...] = jnp.zeros_like(acc)
+
+    @pl.loop(0, DEVS)
+    def _(d):
+        for e in range(1, DEVS):
+
+            @pl.when(d == e)
+            def _():
+                r_copy(e).wait()
+                w_copy(e).wait()
+
+        widen(d)
+        for e in range(1, DEVS):
+
+            @pl.when(d == e)
+            def _():
+                if e in (1, 2, 4, 6):
+                    l_copy(e).wait()
+                    if e > 1:
+                        l_pass(e).start()
+                else:
+                    l_pass(e - 1).wait()
+
+        chunk(0, d, y_buf0, z_buf0, False)
+
+    share(0)
+
+    @pl.loop(1, 2 * STEPS)
     def _(t):
         r, j = lax.rem(t, 2), t // 2
         pr, pj = 1 - r, (t - 1) // 2
@@ -254,10 +270,10 @@
             arrive(r)
 
         for d in range(DEVS):
-            chunk(r, d)
+            chunk(r, d, (y_buf0, y_buf1)[d % 2], (z_buf0, z_buf1)[d % 2], d == 0)
             if d == FORM_AFTER:
 
-                @pl.when(jnp.logical_and(t >= 1, t < 2 * STEPS - 1))
+                @pl.when(t < 2 * STEPS - 1)
                 def _():
                     advance(pr, pj, False)
 
@@ -265,19 +281,22 @@
                 def _():
                     advance(pr, pj, True)
 
+            if d == COLLECT_AFTER:
+
                 @pl.when(t >= 2)
                 def _():
                     collect(r, j - 1)
 
-            if d == RELAY_AFTER:
-
-                @pl.when(jnp.logical_and(t >= 1, t < 2 * STEPS - 1))
-                def _():
-                    relay(pr)
-
         share(r)
 
+        @pl.when(t < 2 * STEPS - 1)
+        def _():
+            relay(pr)
+
+        post(pr)
+
     advance(1, STEPS - 1, True)
+    post(1)
     collect(0, STEPS - 1)
     collect(1, STEPS - 1)
     alpha_ref[...] = numbers[0, 0:2, 0:STEPS]

time: 175 us -> 163 us (0.931)
  Pallas kernels: 168 us -> 157 us
    pallas_call x1, Pallas kernels: 168 us -> 157 us  [device_fn(): pl.pallas_call(kernel, out_shape=(jax.ShapeDtypeStruct((roots, STEPS + 1,...]
where the time goes in v4:
time: 163 us
  Pallas kernels  157 us (96%)
  local copies, waits for them, and re-layouts  5.79 us (4%)
    pallas_call x1, Pallas kernels, device_fn(): pl.pallas_call(kernel, out_shape=(jax.ShapeDtypeStruct((roots, STEPS + 1,...  157 us
    unnamed x7, local copies, waits for them, and re-layouts  4.23 us

profile of v4, /device:TPU:0, one launch (start us, length us, event | category | flops | bytes accessed | tf_op | source)
XLA Modules:
  0.0 163.1 jit_solution(6501565957898769574)
XLA Ops:
  0.6 1.6 reshape.9.phys_ref
  2.2 156.6 %shard_map.67 = (f32[2,7,16,4,4,128]{5,4,3,2,1,0:T(4,128)}, f32[2,6]{1,0:T(2,128)}, f32[2,6]{1,0:T(2,128)}) custom-call(f32[2,128,4,4,128]{4,3,2,1,0:T(4,128)} %psi_ref.1, bf16[16,128,128]{2,1,0:T(8,128)(2,1)} %left_ref.1, bf16[16,128,128]{2,1,0:T(8,128)(2,1)} %right_ref.1, bf16[16,256]{1,0:T(8,128)(2,1)} %reshape.9.phys_ref), custom_call_target="tpu_custom_call" | custom-call | tf_op jit(solution)/shard_map/pallas_call | solution.py:311
  158.8 0.0 copy-start.1
  158.8 0.0 copy-start
  158.9 3.1 %copy.10 = f32[2,7,16,4,4,128]{5,4,3,2,1,0:T(4,128)} copy(f32[2,7,16,4,4,128]{5,4,3,2,1,0:T(4,128)} %get-tuple-element.6) | data formatting | bytes 3670016
  161.9 0.0 copy-done.1
  162.0 0.6 copy.11
  162.5 0.0 copy-done
  162.5 0.6 copy.12
Async XLA Ops:
  158.8 3.1 %copy-start.1 = (f32[2,6]{1,0:T(2,128)S(1)}, f32[2,6]{1,0:T(2,128)}, u32[]{:S(2)}) copy-start(f32[2,6]{1,0:T(2,128)} %get-tuple-element.7) | copy-start | bytes 148
  158.8 3.7 %copy-start = (f32[2,6]{1,0:T(2,128)S(1)}, f32[2,6]{1,0:T(2,128)}, u32[]{:S(2)}) copy-start(f32[2,6]{1,0:T(2,128)} %get-tuple-element.8) | copy-start | bytes 148

commit v5 on v4

--- a/solution.py
+++ b/solution.py
@@ -14,8 +14,8 @@
 BOND = 128
 ROWS = 16
 N_ELEMS = float(BOND * PAIRS * BOND)
-FORM_AFTER = 1
-COLLECT_AFTER = 5
+FORM_BEFORE = 0
+COLLECT_BEFORE = 4
 MESH = pl.DeviceIdType.MESH
 F32 = jnp.float32
 BF16 = jnp.bfloat16
@@ -38,8 +38,8 @@
 
 def kernel(
     psi_ref, left_ref, right_ref, phys_ref, out_ref, alpha_ref, beta_ref,
-    left, right, phys, wide, v_in, y_buf0, y_buf1, z_buf0, z_buf1, acc, sig, v_cur, v_prev, beta_old, stats, mine,
-    turned, got, across, numbers,
+    left, right, phys, wide, v_in, y_buf, z_buf0, z_buf1, acc, sig, v_cur, v_prev, beta_old, stats, mine,
+    turned, got, across, numbers, dense,
     r_send, r_recv, w_send, w_recv, l_send, l_recv, s_send, s_recv, g_send, g_recv, o_send, o_recv,
 ):
     me = lax.axis_index("terms")
@@ -60,7 +60,7 @@
         return copy(right_ref.at[:, rows, :], right.at[e], r_send.at[e], r_recv.at[e], e)
 
     def w_copy(e):
-        return copy(phys_ref, phys.at[e], w_send.at[e], w_recv.at[e], e)
+        return copy(dense, phys.at[e], w_send.at[e], w_recv.at[e], e)
 
     def l_copy(e):
         return copy(left_ref, left.at[e], l_send.at[e], l_recv.at[e], e)
@@ -71,17 +71,26 @@
     def s_copy(r, e):
         return copy(mine.at[r], stats.at[r, me], s_send.at[r, e], s_recv.at[r, e], e)
 
-    def g_copy(r, e):
-        return copy(v_in.at[r, me], v_in.at[r, me], g_send.at[r, e], g_recv.at[r, e], e)
-
-    def g_pass(r, e):
-        slot = v_in.at[r, peers[e]]
-        return copy(slot, slot, g_send.at[r, e + 1], g_recv.at[r, e + 1], 1)
+    def g_copy(r, g, e):
+        slot = v_in.at[r, me, g * 8 : (g + 1) * 8]
+        return copy(slot, slot, g_send.at[r, g, e], g_recv.at[r, g, e], e)
+
+    def g_pass(r, g, e):
+        slot = v_in.at[r, peers[e], g * 8 : (g + 1) * 8]
+        return copy(slot, slot, g_send.at[r, g, e + 1], g_recv.at[r, g, e + 1], 1)
 
     def o_copy(r, e):
         rows = pl.ds(pl.multiple_of(peers[e] * ROWS, ROWS), ROWS)
         return copy(turned.at[r, :, rows, :], got.at[r, me], o_send.at[r, e], o_recv.at[r, e], e)
 
+    w_own = phys_ref[...].astype(F32)
+    row_u = lax.broadcasted_iota(jnp.int32, (PAIRS, PAIRS * PAIRS), 0)
+    col_qu = lax.broadcasted_iota(jnp.int32, (PAIRS, PAIRS * PAIRS), 1)
+    flat = jnp.zeros((TERMS, PAIRS * PAIRS), F32)
+    for q in range(PAIRS):
+        put = jnp.where(col_qu == row_u + q * PAIRS, 1.0, 0.0).astype(BF16)
+        flat += jnp.dot(w_own[:, q, :].astype(BF16), put, preferred_element_type=F32)
+    dense[...] = flat.astype(BF16)
     for both in ((1,), (2, 3), (4, 5), (6, 7)):
         for e in both:
             r_copy(e).start()
@@ -89,7 +98,7 @@
         l_copy(2 * (both[0] // 2) if both[0] > 1 else 1).start()
     own = pl.ds(pl.multiple_of(me * ROWS, ROWS), ROWS)
     right[0] = right_ref[:, own, :]
-    phys[0] = phys_ref[...]
+    phys[0] = dense[...]
     left[0] = left_ref[...]
     v_prev[...] = jnp.zeros_like(v_prev)
     beta_old[...] = jnp.zeros_like(beta_old)
@@ -135,15 +144,17 @@
                 two = [jnp.broadcast_to(spread[q + i][k : k + 1, :], (8, BOND)) * eye for i in range(2)]
                 wide[d, k, q * 8 : q * 8 + 16, :] = jnp.concatenate(two, axis=0).astype(BF16)
 
-    def chunk(r, d, y_buf, z_buf, first):
+    def form_y(r, d, pairs):
         r_d = right[d].reshape(TERMS * ROWS, BOND)
-        for u in range(0, PAIRS, 2):
+        for u in pairs:
             v_u = jnp.concatenate([v_in[r, :, u + i].reshape(BOND, BOND) for i in range(2)], axis=1)
             y = jnp.dot(r_d, v_u, preferred_element_type=F32).reshape(TERMS, 2, 8, 2 * BOND)
             y = jnp.concatenate([y[..., :BOND], y[..., BOND:]], axis=2)
-            y_buf[:, :, u * 8 : u * 8 + 16, :] = y.astype(BF16)
+            y_buf[d, :, :, u * 8 : u * 8 + 16, :] = y.astype(BF16)
+
+    def form_out(d, z_buf, first):
         for k in range(TERMS):
-            y_k = jnp.concatenate([y_buf[k, 0], y_buf[k, 1]], axis=1)
+            y_k = jnp.concatenate([y_buf[d, k, 0], y_buf[d, k, 1]], axis=1)
             z = jnp.dot(wide[d, k], y_k, preferred_element_type=F32).astype(BF16)
             for h in range(2):
                 z_buf[h * BOND : (h + 1) * BOND, k * BOND : (k + 1) * BOND] = z[:, h * BOND : (h + 1) * BOND]
@@ -191,12 +202,14 @@
         numbers[1] = jnp.where(here, beta, numbers[1])
         halves = nxt.reshape(2, PAIRS, 8, BOND)
         joined = jnp.concatenate([halves[0], halves[1]], axis=1)
-        if last:
-            pass
-        else:
+
+        @pl.when(jnp.logical_not(last))
+        def _():
             v_in[r, me] = joined.astype(BF16)
-            for e in (6, 2, 4, 1):
-                g_copy(r, e).start()
+            for g in range(2):
+                for e in (6, 2, 4, 1):
+                    g_copy(r, g, e).start()
+
         for g in range(2):
             turned[r, g] = joined[g * 8 : (g + 1) * 8].reshape(BOND, BOND).T
 
@@ -206,14 +219,15 @@
         got[r, me] = turned[r, :, own, :]
 
     def relay(r):
+        for g in range(2):
+            for e in (4, 6, 2):
+                g_copy(r, g, e).wait()
+                g_pass(r, g, e).start()
+
+    def arrive(r, g):
+        g_copy(r, g, 1).wait()
         for e in (4, 6, 2):
-            g_copy(r, e).wait()
-            g_pass(r, e).start()
-
-    def arrive(r):
-        g_copy(r, 1).wait()
-        for e in (2, 4, 6):
-            g_pass(r, e).wait()
+            g_pass(r, g, e).wait()
 
     def collect(r, j):
         for e in range(1, DEVS):
@@ -256,7 +270,8 @@
                 else:
                     l_pass(e - 1).wait()
 
-        chunk(0, d, y_buf0, z_buf0, False)
+        form_y(0, d, range(0, PAIRS, 2))
+        form_out(d, z_buf0, False)
 
     share(0)
 
@@ -265,28 +280,27 @@
         r, j = lax.rem(t, 2), t // 2
         pr, pj = 1 - r, (t - 1) // 2
 
-        @pl.when(t >= 2)
-        def _():
-            arrive(r)
+        for g in range(2):
+
+            @pl.when(t >= 2)
+            def _():
+                arrive(r, g)
+
+            for u in range(g * 8, (g + 1) * 8, 2):
+                for d in range(DEVS):
+                    form_y(r, d, (u,))
 
         for d in range(DEVS):
-            chunk(r, d, (y_buf0, y_buf1)[d % 2], (z_buf0, z_buf1)[d % 2], d == 0)
-            if d == FORM_AFTER:
-
-                @pl.when(t < 2 * STEPS - 1)
-                def _():
-                    advance(pr, pj, False)
-
-                @pl.when(t == 2 * STEPS - 1)
-                def _():
-                    advance(pr, pj, True)
-
-            if d == COLLECT_AFTER:
+            if d == FORM_BEFORE:
+                advance(pr, pj, t == 2 * STEPS - 1)
+            if d == COLLECT_BEFORE:
 
                 @pl.when(t >= 2)
                 def _():
                     collect(r, j - 1)
 
+            form_out(d, (z_buf0, z_buf1)[d % 2], d == 0)
+
         share(r)
 
         @pl.when(t < 2 * STEPS - 1)
@@ -295,7 +309,7 @@
 
         post(pr)
 
-    advance(1, STEPS - 1, True)
+    advance(1, STEPS - 1, jnp.bool_(True))
     post(1)
     collect(0, STEPS - 1)
     collect(1, STEPS - 1)
@@ -323,8 +337,7 @@
                 pltpu.VMEM((DEVS, TERMS, PAIRS * PAIRS), BF16),
                 pltpu.VMEM((DEVS, TERMS, BOND, BOND), BF16),
                 pltpu.VMEM((roots, DEVS, PAIRS, ROWS, BOND), BF16),
-                pltpu.VMEM((TERMS, 2, BOND, BOND), BF16),
-                pltpu.VMEM((TERMS, 2, BOND, BOND), BF16),
+                pltpu.VMEM((DEVS, TERMS, 2, BOND, BOND), BF16),
                 pltpu.VMEM((2 * BOND, TERMS * BOND), BF16),
                 pltpu.VMEM((2 * BOND, TERMS * BOND), BF16),
                 pltpu.VMEM((2 * BOND, BOND), F32),
@@ -338,14 +351,15 @@
                 pltpu.VMEM((roots, DEVS, 2, ROWS, BOND), F32),
                 pltpu.VMEM((PAIRS, BOND, BOND), F32),
                 pltpu.VMEM((2, 8, BOND), F32),
+                pltpu.VMEM((TERMS, PAIRS * PAIRS), BF16),
                 dma((DEVS,)), dma((DEVS,)), dma((DEVS,)), dma((DEVS,)), dma((DEVS,)), dma((DEVS,)),
-                dma((roots, DEVS)), dma((roots, DEVS)), dma((roots, DEVS)), dma((roots, DEVS)),
+                dma((roots, DEVS)), dma((roots, DEVS)), dma((roots, 2, DEVS)), dma((roots, 2, DEVS)),
                 dma((roots, DEVS)), dma((roots, DEVS)),
             ],
             compiler_params=pltpu.CompilerParams(
                 collective_id=0, has_side_effects=True, vmem_limit_bytes=56 * 1024 * 1024
             ),
-        )(psi, left_loc, right_loc, phys_loc.reshape(TERMS, PAIRS * PAIRS))
+        )(psi, left_loc, right_loc, phys_loc)
 
     return jax.shard_map(
         device_fn, mesh=mesh, in_specs=(P(), P("terms"), P("terms"), P("terms")),

time: 163 us -> 154 us (0.945)
  Pallas kernels: 157 us -> 149 us
    pallas_call x1, Pallas kernels: 157 us -> 149 us  [device_fn(): pl.pallas_call(kernel, out_shape=(jax.ShapeDtypeStruct((roots, STEPS + 1,...]
where the time goes in v5:
time: 154 us; the launch traced here: 153 us
  Pallas kernels  149 us (97%)
  local copies, waits for them, and re-layouts  4.23 us (3%)
    pallas_call x1, Pallas kernels, device_fn(): pl.pallas_call(kernel, out_shape=(jax.ShapeDtypeStruct((roots, STEPS + 1,...  149 us
    unnamed x7, local copies, waits for them, and re-layouts  4.23 us

profile of v5, /device:TPU:0, one launch (start us, length us, event | category | flops | bytes accessed | tf_op | source)
XLA Modules:
  0.0 153.4 jit_solution(7676353319912422455)
XLA Ops:
  0.6 148.5 %shard_map.67 = (f32[2,7,16,4,4,128]{5,4,3,2,1,0:T(4,128)}, f32[2,6]{1,0:T(2,128)}, f32[2,6]{1,0:T(2,128)}) custom-call(f32[2,128,4,4,128]{4,3,2,1,0:T(4,128)} %psi_ref.1, bf16[16,128,128]{2,1,0:T(8,128)(2,1)} %left_ref.1, bf16[16,128,128]{2,1,0:T(8,128)(2,1)} %right_ref.1, bf16[16,16,16]{2,1,0:T(8,128)(2,1)} %phys_ref.1), custom_call_target="tpu_custom_call" | custom-call | tf_op jit(solution)/shard_map/pallas_call | solution.py:325
  149.2 0.0 copy-start.1
  149.2 0.0 copy-start
  149.2 3.1 %copy.10 = f32[2,7,16,4,4,128]{5,4,3,2,1,0:T(4,128)} copy(f32[2,7,16,4,4,128]{5,4,3,2,1,0:T(4,128)} %get-tuple-element.6) | data formatting | bytes 3670016
  152.3 0.0 copy-done.1
  152.3 0.6 copy.11
  152.8 0.0 copy-done
  152.8 0.6 copy.12
Async XLA Ops:
  149.2 3.1 %copy-start.1 = (f32[2,6]{1,0:T(2,128)S(1)}, f32[2,6]{1,0:T(2,128)}, u32[]{:S(2)}) copy-start(f32[2,6]{1,0:T(2,128)} %get-tuple-element.7) | copy-start | bytes 148
  149.2 3.7 %copy-start = (f32[2,6]{1,0:T(2,128)S(1)}, f32[2,6]{1,0:T(2,128)}, u32[]{:S(2)}) copy-start(f32[2,6]{1,0:T(2,128)} %get-tuple-element.8) | copy-start | bytes 148

commit v6 on v5

--- a/solution.py
+++ b/solution.py
@@ -16,6 +16,7 @@
 N_ELEMS = float(BOND * PAIRS * BOND)
 FORM_BEFORE = 0
 COLLECT_BEFORE = 4
+POST_BEFORE = 6
 MESH = pl.DeviceIdType.MESH
 F32 = jnp.float32
 BF16 = jnp.bfloat16
@@ -39,8 +40,8 @@
 def kernel(
     psi_ref, left_ref, right_ref, phys_ref, out_ref, alpha_ref, beta_ref,
     left, right, phys, wide, v_in, y_buf, z_buf0, z_buf1, acc, sig, v_cur, v_prev, beta_old, stats, mine,
-    turned, got, across, numbers, dense,
-    r_send, r_recv, w_send, w_recv, l_send, l_recv, s_send, s_recv, g_send, g_recv, o_send, o_recv,
+    turned, got, got_end, across, numbers, dense,
+    r_send, r_recv, w_send, w_recv, l_send, l_recv, s_send, s_recv, g_send, g_recv, o_send, o_recv, e_send, e_recv,
 ):
     me = lax.axis_index("terms")
     peers = {e: flip(me, e) for e in range(1, DEVS)}
@@ -62,11 +63,18 @@
     def w_copy(e):
         return copy(dense, phys.at[e], w_send.at[e], w_recv.at[e], e)
 
-    def l_copy(e):
-        return copy(left_ref, left.at[e], l_send.at[e], l_recv.at[e], e)
-
-    def l_pass(e):
-        return copy(left.at[e], left.at[e + 1], l_send.at[e + 1], l_recv.at[e + 1], 1)
+    def half(x):
+        return pl.ds(x * (TERMS // 2), TERMS // 2)
+
+    def l_copy(e, x):
+        return copy(left_ref.at[half(x)], left.at[e, half(x)], l_send.at[e, x], l_recv.at[e, x], e)
+
+    def l_far(x):
+        e = (2, 4)[x]
+        return copy(left.at[e, half(x)], left.at[6, half(x)], l_send.at[6, x], l_recv.at[6, x], 6 - e)
+
+    def l_pass(e, x):
+        return copy(left.at[e, half(x)], left.at[e + 1, half(x)], l_send.at[e + 1, x], l_recv.at[e + 1, x], 1)
 
     def s_copy(r, e):
         return copy(mine.at[r], stats.at[r, me], s_send.at[r, e], s_recv.at[r, e], e)
@@ -82,6 +90,10 @@
     def o_copy(r, e):
         rows = pl.ds(pl.multiple_of(peers[e] * ROWS, ROWS), ROWS)
         return copy(turned.at[r, :, rows, :], got.at[r, me], o_send.at[r, e], o_recv.at[r, e], e)
+
+    def e_copy(e):
+        rows = pl.ds(pl.multiple_of(peers[e] * ROWS, ROWS), ROWS)
+        return copy(turned.at[1, :, rows, :], got_end.at[me], e_send.at[e], e_recv.at[e], e)
 
     w_own = phys_ref[...].astype(F32)
     row_u = lax.broadcasted_iota(jnp.int32, (PAIRS, PAIRS * PAIRS), 0)
@@ -91,11 +103,11 @@
         put = jnp.where(col_qu == row_u + q * PAIRS, 1.0, 0.0).astype(BF16)
         flat += jnp.dot(w_own[:, q, :].astype(BF16), put, preferred_element_type=F32)
     dense[...] = flat.astype(BF16)
-    for both in ((1,), (2, 3), (4, 5), (6, 7)):
-        for e in both:
-            r_copy(e).start()
-            w_copy(e).start()
-        l_copy(2 * (both[0] // 2) if both[0] > 1 else 1).start()
+    for e in (6, 7, 2, 3, 4, 5, 1):
+        r_copy(e).start()
+        w_copy(e).start()
+    for e, x in ((1, 0), (1, 1), (2, 0), (4, 1), (2, 1), (4, 0)):
+        l_copy(e, x).start()
     own = pl.ds(pl.multiple_of(me * ROWS, ROWS), ROWS)
     right[0] = right_ref[:, own, :]
     phys[0] = dense[...]
@@ -179,7 +191,7 @@
         for e in (6, 7, 2, 3, 4, 5, 1):
             s_copy(r, e).start()
 
-    def advance(r, j, last):
+    def scalars(r, j):
         for e in range(1, DEVS):
             s_copy(r, e).wait()
         alpha = jnp.zeros((1, BOND), F32)
@@ -191,15 +203,23 @@
             d_p = alpha - stats[r, p, 2:3, :]
             square = square + (stats[r, p, 3:4, :] - 2.0 * d_p * stats[r, p, 4:5, :] + d_p * d_p * stats[r, p, 1:2, :])
         beta = jnp.sqrt(jnp.maximum(square, 0.0) / N_ELEMS)
+        here = jnp.logical_and(sub == r, lane == j)
+        numbers[0] = jnp.where(here, alpha, numbers[0])
+        numbers[1] = jnp.where(here, beta, numbers[1])
+        return alpha, beta
+
+    def turn(r, joined):
+        for g in range(2):
+            turned[r, g] = joined[g * 8 : (g + 1) * 8].reshape(BOND, BOND).T
+
+    def advance(r, j, last):
+        alpha, beta = scalars(r, j)
         shift = alpha - mine[r, 2:3, :]
         v = v_cur[r]
         nxt = (sig[r] - shift * v) / beta
         v_prev[r] = v
         v_cur[r] = nxt
         beta_old[r] = jnp.broadcast_to(beta, (8, BOND))
-        here = jnp.logical_and(sub == r, lane == j)
-        numbers[0] = jnp.where(here, alpha, numbers[0])
-        numbers[1] = jnp.where(here, beta, numbers[1])
         halves = nxt.reshape(2, PAIRS, 8, BOND)
         joined = jnp.concatenate([halves[0], halves[1]], axis=1)
 
@@ -210,8 +230,7 @@
                 for e in (6, 2, 4, 1):
                     g_copy(r, g, e).start()
 
-        for g in range(2):
-            turned[r, g] = joined[g * 8 : (g + 1) * 8].reshape(BOND, BOND).T
+        turn(r, joined)
 
     def post(r):
         for e in (6, 7, 2, 3, 4, 5, 1):
@@ -229,12 +248,11 @@
         for e in (4, 6, 2):
             g_pass(r, g, e).wait()
 
-    def collect(r, j):
-        for e in range(1, DEVS):
-            o_copy(r, e).wait()
+    def assemble(read):
         chunk_of = lax.broadcasted_iota(jnp.int32, (ROWS, BOND), 1) // 16
+        pairs = []
         for g in range(2):
-            x = [got[r, p, g] for p in range(DEVS)]
+            x = [read(p, g) for p in range(DEVS)]
             for bit in (1, 2, 4):
                 odd = lax.rem(chunk_of // bit, 2) == 1
                 for p in range(DEVS):
@@ -243,9 +261,14 @@
                     low, high = x[p], x[p + bit]
                     x[p] = jnp.where(odd, pltpu.roll(high, 16 * bit, 1), low)
                     x[p + bit] = jnp.where(odd, high, pltpu.roll(low, BOND - 16 * bit, 1))
-            for q in range(8):
-                pair = g * 8 + q
-                out_ref[r, j + 1, :, pair // 4, pair % 4, :] = x[q]
+            pairs += x
+        return pairs
+
+    def collect(r, j):
+        for e in range(1, DEVS):
+            o_copy(r, e).wait()
+        for q, x in enumerate(assemble(lambda p, g: got[r, p, g])):
+            out_ref[r, j + 1, :, q // 4, q % 4, :] = x
 
     acc[...] = jnp.zeros_like(acc)
 
@@ -259,18 +282,38 @@
                 w_copy(e).wait()
 
         widen(d)
-        for e in range(1, DEVS):
+        form_y(0, d, range(0, PAIRS, 2))
+
+    @pl.loop(0, DEVS)
+    def _(d):
+        @pl.when(d == 1)
+        def _():
+            l_copy(1, 0).wait()
+            l_copy(1, 1).wait()
+
+        @pl.when(d == 2)
+        def _():
+            for e, x in ((2, 0), (4, 1)):
+                l_copy(e, x).wait()
+                l_far(x).start()
+                l_pass(e, x).start()
+            for e, x in ((2, 1), (4, 0)):
+                l_copy(e, x).wait()
+                l_pass(e, x).start()
+
+        @pl.when(d == 6)
+        def _():
+            for x in range(2):
+                l_far(x).wait()
+                l_pass(6, x).start()
+
+        for e in (3, 5, 7):
 
             @pl.when(d == e)
             def _():
-                if e in (1, 2, 4, 6):
-                    l_copy(e).wait()
-                    if e > 1:
-                        l_pass(e).start()
-                else:
-                    l_pass(e - 1).wait()
-
-        form_y(0, d, range(0, PAIRS, 2))
+                for x in range(2):
+                    l_pass(e - 1, x).wait()
+
         form_out(d, z_buf0, False)
 
     share(0)
@@ -299,6 +342,8 @@
                 def _():
                     collect(r, j - 1)
 
+            if d == POST_BEFORE:
+                post(pr)
             form_out(d, (z_buf0, z_buf1)[d % 2], d == 0)
 
         share(r)
@@ -307,12 +352,21 @@
         def _():
             relay(pr)
 
-        post(pr)
-
-    advance(1, STEPS - 1, jnp.bool_(True))
-    post(1)
+    halves = sig[1].reshape(2, PAIRS, 8, BOND)
+    turn(1, jnp.concatenate([halves[0], halves[1]], axis=1))
+    for e in (6, 7, 2, 3, 4, 5, 1):
+        e_copy(e).start()
+    got_end[me] = turned[1, :, own, :]
     collect(0, STEPS - 1)
-    collect(1, STEPS - 1)
+    alpha, beta = scalars(1, STEPS - 1)
+    shift = jnp.zeros((1, BOND), F32)
+    for p in range(DEVS):
+        shift = jnp.where(lane[0:1] // 16 == p, alpha - stats[1, p, 2:3, :], shift)
+    for e in range(1, DEVS):
+        e_copy(e).wait()
+    for q, x in enumerate(assemble(lambda p, g: got_end[p, g])):
+        v = out_ref[1, STEPS - 1, :, q // 4, q % 4, :]
+        out_ref[1, STEPS, :, q // 4, q % 4, :] = (x - shift * v) / beta
     alpha_ref[...] = numbers[0, 0:2, 0:STEPS]
     beta_ref[...] = numbers[1, 0:2, 0:STEPS]
 
@@ -349,12 +403,13 @@
                 pltpu.VMEM((roots, 8, BOND), F32),
                 pltpu.VMEM((roots, 2, BOND, BOND), F32),
                 pltpu.VMEM((roots, DEVS, 2, ROWS, BOND), F32),
+                pltpu.VMEM((DEVS, 2, ROWS, BOND), F32),
                 pltpu.VMEM((PAIRS, BOND, BOND), F32),
                 pltpu.VMEM((2, 8, BOND), F32),
                 pltpu.VMEM((TERMS, PAIRS * PAIRS), BF16),
-                dma((DEVS,)), dma((DEVS,)), dma((DEVS,)), dma((DEVS,)), dma((DEVS,)), dma((DEVS,)),
+                dma((DEVS,)), dma((DEVS,)), dma((DEVS,)), dma((DEVS,)), dma((DEVS, 2)), dma((DEVS, 2)),
                 dma((roots, DEVS)), dma((roots, DEVS)), dma((roots, 2, DEVS)), dma((roots, 2, DEVS)),
-                dma((roots, DEVS)), dma((roots, DEVS)),
+                dma((roots, DEVS)), dma((roots, DEVS)), dma((DEVS,)), dma((DEVS,)),
             ],
             compiler_params=pltpu.CompilerParams(
                 collective_id=0, has_side_effects=True, vmem_limit_bytes=56 * 1024 * 1024

time: 154 us -> 144 us (0.935)
  Pallas kernels: 149 us -> 139 us
    pallas_call x1, Pallas kernels: 149 us -> 139 us  [device_fn(): pl.pallas_call(kernel, out_shape=(jax.ShapeDtypeStruct((roots, STEPS + 1,...]
where the time goes in v6:
time: 144 us
  Pallas kernels  139 us (97%)
  local copies, waits for them, and re-layouts  4.23 us (3%)
    pallas_call x1, Pallas kernels, device_fn(): pl.pallas_call(kernel, out_shape=(jax.ShapeDtypeStruct((roots, STEPS + 1,...  139 us
    unnamed x7, local copies, waits for them, and re-layouts  4.23 us

profile of v6, /device:TPU:0, one launch (start us, length us, event | category | flops | bytes accessed | tf_op | source)
XLA Modules:
  0.0 144.2 jit_solution(11806708534677724201)
XLA Ops:
  0.6 139.3 %shard_map.67 = (f32[2,7,16,4,4,128]{5,4,3,2,1,0:T(4,128)}, f32[2,6]{1,0:T(2,128)}, f32[2,6]{1,0:T(2,128)}) custom-call(f32[2,128,4,4,128]{4,3,2,1,0:T(4,128)} %psi_ref.1, bf16[16,128,128]{2,1,0:T(8,128)(2,1)} %left_ref.1, bf16[16,128,128]{2,1,0:T(8,128)(2,1)} %right_ref.1, bf16[16,16,16]{2,1,0:T(8,128)(2,1)} %phys_ref.1), custom_call_target="tpu_custom_call" | custom-call | tf_op jit(solution)/shard_map/pallas_call | solution.py:379
  139.9 0.0 copy-start.1
  139.9 0.0 copy-start
  139.9 3.1 %copy.10 = f32[2,7,16,4,4,128]{5,4,3,2,1,0:T(4,128)} copy(f32[2,7,16,4,4,128]{5,4,3,2,1,0:T(4,128)} %get-tuple-element.6) | data formatting | bytes 3670016
  143.0 0.0 copy-done.1
  143.0 0.6 copy.11
  143.6 0.0 copy-done
  143.6 0.6 copy.12
Async XLA Ops:
  139.9 3.1 %copy-start.1 = (f32[2,6]{1,0:T(2,128)S(1)}, f32[2,6]{1,0:T(2,128)}, u32[]{:S(2)}) copy-start(f32[2,6]{1,0:T(2,128)} %get-tuple-element.7) | copy-start | bytes 148
  139.9 3.7 %copy-start = (f32[2,6]{1,0:T(2,128)S(1)}, f32[2,6]{1,0:T(2,128)}, u32[]{:S(2)}) copy-start(f32[2,6]{1,0:T(2,128)} %get-tuple-element.8) | copy-start | bytes 148

commit v7 on v6

--- a/solution.py
+++ b/solution.py
@@ -38,18 +38,17 @@
 
 
 def kernel(
-    psi_ref, left_ref, right_ref, phys_ref, out_ref, alpha_ref, beta_ref,
+    psi_hbm, left_ref, right_ref, phys_ref, out_ref, alpha_ref, beta_ref, scale_ref,
     left, right, phys, wide, v_in, y_buf, z_buf0, z_buf1, acc, sig, v_cur, v_prev, beta_old, stats, mine,
-    turned, got, got_end, across, numbers, dense,
+    turned, got, got_end, across, numbers, dense, psi_ref, psi_sem,
     r_send, r_recv, w_send, w_recv, l_send, l_recv, s_send, s_recv, g_send, g_recv, o_send, o_recv, e_send, e_recv,
 ):
     me = lax.axis_index("terms")
     peers = {e: flip(me, e) for e in range(1, DEVS)}
 
-    barrier = pltpu.get_barrier_semaphore()
-    for e in range(1, DEVS):
-        pl.semaphore_signal(barrier, inc=1, device_id=(peers[e],), device_id_type=MESH)
-    pl.semaphore_wait(barrier, DEVS - 1)
+    psi_copies = [pltpu.make_async_copy(psi_hbm.at[r], psi_ref.at[r], psi_sem.at[r]) for r in range(2)]
+    for psi_copy in psi_copies:
+        psi_copy.start()
 
     def copy(src, dst, send, recv, e):
         return pltpu.make_async_remote_copy(
@@ -103,7 +102,12 @@
         put = jnp.where(col_qu == row_u + q * PAIRS, 1.0, 0.0).astype(BF16)
         flat += jnp.dot(w_own[:, q, :].astype(BF16), put, preferred_element_type=F32)
     dense[...] = flat.astype(BF16)
-    for e in (6, 7, 2, 3, 4, 5, 1):
+    barrier = pltpu.get_barrier_semaphore()
+    for e in range(1, DEVS):
+        pl.semaphore_signal(barrier, inc=1, device_id=(peers[e],), device_id_type=MESH)
+    pl.semaphore_wait(barrier, DEVS - 1)
+
+    for e in (1, 2, 4, 3, 5, 6, 7):
         r_copy(e).start()
         w_copy(e).start()
     for e, x in ((1, 0), (1, 1), (2, 0), (4, 1), (2, 1), (4, 0)):
@@ -115,6 +119,9 @@
     v_prev[...] = jnp.zeros_like(v_prev)
     beta_old[...] = jnp.zeros_like(beta_old)
     numbers[...] = jnp.zeros_like(numbers)
+
+    for psi_copy in psi_copies:
+        psi_copy.wait()
 
     @pl.loop(0, 2)
     def _(r):
@@ -227,7 +234,7 @@
         def _():
             v_in[r, me] = joined.astype(BF16)
             for g in range(2):
-                for e in (6, 2, 4, 1):
+                for e in (6, 4, 2, 1):
                     g_copy(r, g, e).start()
 
         turn(r, joined)
@@ -366,9 +373,11 @@
         e_copy(e).wait()
     for q, x in enumerate(assemble(lambda p, g: got_end[p, g])):
         v = out_ref[1, STEPS - 1, :, q // 4, q % 4, :]
-        out_ref[1, STEPS, :, q // 4, q % 4, :] = (x - shift * v) / beta
+        out_ref[1, STEPS, :, q // 4, q % 4, :] = x - shift * v
     alpha_ref[...] = numbers[0, 0:2, 0:STEPS]
     beta_ref[...] = numbers[1, 0:2, 0:STEPS]
+    end = jnp.logical_and(sub == 1, lane == STEPS)
+    scale_ref[...] = jnp.where(end, 1.0 / beta, jnp.ones((8, BOND), F32))[0:2, 0 : STEPS + 1]
 
 
 def solution(mesh):
@@ -376,15 +385,16 @@
         roots = psi.shape[0]
         vm = pl.BlockSpec(memory_space=pltpu.VMEM)
         dma = pltpu.SemaphoreType.DMA
-        return pl.pallas_call(
+        vecs, alpha, beta, scale = pl.pallas_call(
             kernel,
             out_shape=(
                 jax.ShapeDtypeStruct((roots, STEPS + 1, ROWS) + psi.shape[2:], F32),
                 jax.ShapeDtypeStruct((roots, STEPS), F32),
                 jax.ShapeDtypeStruct((roots, STEPS), F32),
+                jax.ShapeDtypeStruct((roots, STEPS + 1), F32),
             ),
-            in_specs=[vm] * 4,
-            out_specs=(vm, vm, vm),
+            in_specs=[pl.BlockSpec(memory_space=pl.ANY), vm, vm, vm],
+            out_specs=(vm, vm, vm, vm),
             scratch_shapes=[
                 pltpu.VMEM((DEVS, TERMS, BOND, BOND), BF16),
                 pltpu.VMEM((DEVS, TERMS, ROWS, BOND), BF16),
@@ -407,6 +417,8 @@
                 pltpu.VMEM((PAIRS, BOND, BOND), F32),
                 pltpu.VMEM((2, 8, BOND), F32),
                 pltpu.VMEM((TERMS, PAIRS * PAIRS), BF16),
+                pltpu.VMEM(psi.shape, F32),
+                dma((roots,)),
                 dma((DEVS,)), dma((DEVS,)), dma((DEVS,)), dma((DEVS,)), dma((DEVS, 2)), dma((DEVS, 2)),
                 dma((roots, DEVS)), dma((roots, DEVS)), dma((roots, 2, DEVS)), dma((roots, 2, DEVS)),
                 dma((roots, DEVS)), dma((roots, DEVS)), dma((DEVS,)), dma((DEVS,)),
@@ -415,6 +427,7 @@
                 collective_id=0, has_side_effects=True, vmem_limit_bytes=56 * 1024 * 1024
             ),
         )(psi, left_loc, right_loc, phys_loc)
+        return vecs * scale[:, :, None, None, None, None], alpha, beta
 
     return jax.shard_map(
         device_fn, mesh=mesh, in_specs=(P(), P("terms"), P("terms"), P("terms")),

time: 144 us -> 144 us (level)
  other arithmetic: 0 us -> 3.21 us
  local copies, waits for them, and re-layouts: 4.23 us -> 1.13 us
    mul x0 -> x1, other arithmetic: none -> 3.21 us  [device_fn(): return (vecs * scale[:, :, None, None, None, None], alpha, beta)]
    unnamed x7 -> x6, local copies, waits for them, and re-layouts: 4.23 us -> 1.13 us
where the time goes in v7:
time: 144 us
  Pallas kernels  139 us (97%)
  other arithmetic  3.21 us (2%)
    pallas_call x1, Pallas kernels, device_fn(): pl.pallas_call(kernel, out_shape=(jax.ShapeDtypeStruct((roots, STEPS + 1,...  139 us
    mul x1, other arithmetic, device_fn(): return (vecs * scale[:, :, None, None, None, None], alpha, beta)  3.21 us

profile of v7, /device:TPU:0, one launch (start us, length us, event | category | flops | bytes accessed | tf_op | source)
XLA Modules:
  0.0 143.8 jit_solution(4555521967424178267)
XLA Ops:
  0.6 138.8 %shard_map.67 = (f32[2,7,16,4,4,128]{5,4,3,2,1,0:T(4,128)}, f32[2,6]{1,0:T(2,128)}, f32[2,6]{1,0:T(2,128)}, f32[2,7]{1,0:T(2,128)}) custom-call(f32[2,128,4,4,128]{4,3,2,1,0:T(4,128)} %psi_hbm.1, bf16[16,128,128]{2,1,0:T(8,128)(2,1)} %left_ref.1, bf16[16,128,128]{2,1,0:T(8,128)(2,1)} %right_ref.1, bf16[16,16,16]{2,1,0:T(8,128)(2,1)} %phys_ref.1), custom_call_target="tpu_custom_call" | custom-call | tf_op jit(solution)/shard_map/pallas_call | solution.py:388
  139.4 0.0 copy-start.1
  139.4 0.0 copy-start
  139.4 3.2 %broadcast_multiply_fusion = f32[2,7,16,4,4,128]{5,4,3,2,1,0:T(4,128)} fusion(f32[2,7,16,4,4,128]{5,4,3,2,1,0:T(4,128)} %get-tuple-element.7, f32[2,7]{1,0:T(2,128)} %get-tuple-element.8), kind=kLoop, calls=%fused_computation | loop fusion | flops 458752 | bytes 3670072 | tf_op jit(solution)/shard_map/mul | solution.py:430
  142.6 0.0 copy-done.1
  142.7 0.6 copy.9
  143.2 0.0 copy-done
  143.2 0.6 copy.10
Async XLA Ops:
  139.4 3.2 %copy-start.1 = (f32[2,6]{1,0:T(2,128)S(1)}, f32[2,6]{1,0:T(2,128)}, u32[]{:S(2)}) copy-start(f32[2,6]{1,0:T(2,128)} %get-tuple-element.15) | copy-start | bytes 148
  139.4 3.8 %copy-start = (f32[2,6]{1,0:T(2,128)S(1)}, f32[2,6]{1,0:T(2,128)}, u32[]{:S(2)}) copy-start(f32[2,6]{1,0:T(2,128)} %get-tuple-element.16) | copy-start | bytes 148

commit v8 on v7

--- a/solution.py
+++ b/solution.py
@@ -12,6 +12,7 @@
 TERMS = 16
 PAIRS = 16
 BOND = 128
+PACKED = TERMS // 2 * BOND + 16
 ROWS = 16
 N_ELEMS = float(BOND * PAIRS * BOND)
 FORM_BEFORE = 0
@@ -38,9 +39,9 @@
 
 
 def kernel(
-    psi_hbm, left_ref, right_ref, phys_ref, out_ref, alpha_ref, beta_ref, scale_ref,
+    psi_hbm, left_ref, right_ref, phys_ref, out_ref, alpha_ref, beta_ref,
     left, right, phys, wide, v_in, y_buf, z_buf0, z_buf1, acc, sig, v_cur, v_prev, beta_old, stats, mine,
-    turned, got, got_end, across, numbers, dense, psi_ref, psi_sem,
+    turned, got, got_end, across, numbers, dense, psi_ref, psi_sem, tri,
     r_send, r_recv, w_send, w_recv, l_send, l_recv, s_send, s_recv, g_send, g_recv, o_send, o_recv, e_send, e_recv,
 ):
     me = lax.axis_index("terms")
@@ -62,18 +63,18 @@
     def w_copy(e):
         return copy(dense, phys.at[e], w_send.at[e], w_recv.at[e], e)
 
-    def half(x):
-        return pl.ds(x * (TERMS // 2), TERMS // 2)
+    def part(x):
+        return slice(0, 512) if x == 0 else slice(512, PACKED)
 
     def l_copy(e, x):
-        return copy(left_ref.at[half(x)], left.at[e, half(x)], l_send.at[e, x], l_recv.at[e, x], e)
+        return copy(tri.at[0, part(x)], tri.at[e, part(x)], l_send.at[e, x], l_recv.at[e, x], e)
 
     def l_far(x):
         e = (2, 4)[x]
-        return copy(left.at[e, half(x)], left.at[6, half(x)], l_send.at[6, x], l_recv.at[6, x], 6 - e)
+        return copy(tri.at[e, part(x)], tri.at[6, part(x)], l_send.at[6, x], l_recv.at[6, x], 6 - e)
 
     def l_pass(e, x):
-        return copy(left.at[e, half(x)], left.at[e + 1, half(x)], l_send.at[e + 1, x], l_recv.at[e + 1, x], 1)
+        return copy(tri.at[e, part(x)], tri.at[e + 1, part(x)], l_send.at[e + 1, x], l_recv.at[e + 1, x], 1)
 
     def s_copy(r, e):
         return copy(mine.at[r], stats.at[r, me], s_send.at[r, e], s_recv.at[r, e], e)
@@ -93,6 +94,26 @@
     def e_copy(e):
         rows = pl.ds(pl.multiple_of(peers[e] * ROWS, ROWS), ROWS)
         return copy(turned.at[1, :, rows, :], got_end.at[me], e_send.at[e], e_recv.at[e], e)
+
+    row = lax.broadcasted_iota(jnp.int32, (BOND, BOND), 0)
+    col = lax.broadcasted_iota(jnp.int32, (BOND, BOND), 1)
+    diag_row = lax.broadcasted_iota(jnp.int32, (16, BOND), 0)
+    diags = jnp.zeros((16, BOND), F32)
+    for i in range(TERMS // 2):
+        one, two = left_ref[2 * i].astype(F32), left_ref[2 * i + 1].astype(F32)
+        tri[0, i * BOND : (i + 1) * BOND, :] = jnp.where(row < col, one, two).astype(BF16)
+        diag = jnp.sum(jnp.where(row == col, one, 0.0), axis=0, keepdims=True)
+        diags = jnp.where(diag_row == i, diag, diags)
+    tri[0, PACKED - 16 : PACKED, :] = diags.astype(BF16)
+
+    def unpack(d):
+        diags = tri[d, PACKED - 16 : PACKED, :].astype(F32)
+        for i in range(TERMS // 2):
+            m = tri[d, i * BOND : (i + 1) * BOND, :].astype(F32)
+            turned_m = m.T
+            one = jnp.where(row < col, m, jnp.where(row > col, turned_m, diags[i : i + 1, :]))
+            left[d, 2 * i] = one.astype(BF16)
+            left[d, 2 * i + 1] = jnp.where(row < col, turned_m, m).astype(BF16)
 
     w_own = phys_ref[...].astype(F32)
     row_u = lax.broadcasted_iota(jnp.int32, (PAIRS, PAIRS * PAIRS), 0)
@@ -321,6 +342,10 @@
                 for x in range(2):
                     l_pass(e - 1, x).wait()
 
+        @pl.when(d >= 1)
+        def _():
+            unpack(d)
+
         form_out(d, z_buf0, False)
 
     share(0)
@@ -373,11 +398,9 @@
         e_copy(e).wait()
     for q, x in enumerate(assemble(lambda p, g: got_end[p, g])):
         v = out_ref[1, STEPS - 1, :, q // 4, q % 4, :]
-        out_ref[1, STEPS, :, q // 4, q % 4, :] = x - shift * v
+        out_ref[1, STEPS, :, q // 4, q % 4, :] = (x - shift * v) / beta
     alpha_ref[...] = numbers[0, 0:2, 0:STEPS]
     beta_ref[...] = numbers[1, 0:2, 0:STEPS]
-    end = jnp.logical_and(sub == 1, lane == STEPS)
-    scale_ref[...] = jnp.where(end, 1.0 / beta, jnp.ones((8, BOND), F32))[0:2, 0 : STEPS + 1]
 
 
 def solution(mesh):
@@ -385,16 +408,15 @@
         roots = psi.shape[0]
         vm = pl.BlockSpec(memory_space=pltpu.VMEM)
         dma = pltpu.SemaphoreType.DMA
-        vecs, alpha, beta, scale = pl.pallas_call(
+        return pl.pallas_call(
             kernel,
             out_shape=(
                 jax.ShapeDtypeStruct((roots, STEPS + 1, ROWS) + psi.shape[2:], F32),
                 jax.ShapeDtypeStruct((roots, STEPS), F32),
                 jax.ShapeDtypeStruct((roots, STEPS), F32),
-                jax.ShapeDtypeStruct((roots, STEPS + 1), F32),
             ),
             in_specs=[pl.BlockSpec(memory_space=pl.ANY), vm, vm, vm],
-            out_specs=(vm, vm, vm, vm),
+            out_specs=(vm, vm, vm),
             scratch_shapes=[
                 pltpu.VMEM((DEVS, TERMS, BOND, BOND), BF16),
                 pltpu.VMEM((DEVS, TERMS, ROWS, BOND), BF16),
@@ -419,6 +441,7 @@
                 pltpu.VMEM((TERMS, PAIRS * PAIRS), BF16),
                 pltpu.VMEM(psi.shape, F32),
                 dma((roots,)),
+                pltpu.VMEM((DEVS, PACKED, BOND), BF16),
                 dma((DEVS,)), dma((DEVS,)), dma((DEVS,)), dma((DEVS,)), dma((DEVS, 2)), dma((DEVS, 2)),
                 dma((roots, DEVS)), dma((roots, DEVS)), dma((roots, 2, DEVS)), dma((roots, 2, DEVS)),
                 dma((roots, DEVS)), dma((roots, DEVS)), dma((DEVS,)), dma((DEVS,)),
@@ -427,7 +450,6 @@
                 collective_id=0, has_side_effects=True, vmem_limit_bytes=56 * 1024 * 1024
             ),
         )(psi, left_loc, right_loc, phys_loc)
-        return vecs * scale[:, :, None, None, None, None], alpha, beta
 
     return jax.shard_map(
         device_fn, mesh=mesh, in_specs=(P(), P("terms"), P("terms"), P("terms")),

time: 144 us -> 137 us (0.951)
  Pallas kernels: 139 us -> 132 us
  other arithmetic: 3.21 us -> 0 us
  local copies, waits for them, and re-layouts: 1.13 us -> 4.23 us
    pallas_call x1, Pallas kernels: 139 us -> 132 us  [device_fn(): pl.pallas_call(kernel, out_shape=(jax.ShapeDtypeStruct((roots, STEPS + 1,...]
    mul x1 -> x0, other arithmetic: 3.21 us -> none  [device_fn(): return (vecs * scale[:, :, None, None, None, None], alpha, beta)]
    unnamed x6 -> x7, local copies, waits for them, and re-layouts: 1.13 us -> 4.23 us
where the time goes in v8:
time: 137 us
  Pallas kernels  132 us (96%)
  local copies, waits for them, and re-layouts  4.23 us (3%)
    pallas_call x1, Pallas kernels, device_fn(): pl.pallas_call(kernel, out_shape=(jax.ShapeDtypeStruct((roots, STEPS + 1,...  132 us
    unnamed x7, local copies, waits for them, and re-layouts  4.23 us

profile of v8, /device:TPU:0, one launch (start us, length us, event | category | flops | bytes accessed | tf_op | source)
XLA Modules:
  0.0 137.2 jit_solution(1240414463347503123)
XLA Ops:
  0.6 132.3 %shard_map.67 = (f32[2,7,16,4,4,128]{5,4,3,2,1,0:T(4,128)}, f32[2,6]{1,0:T(2,128)}, f32[2,6]{1,0:T(2,128)}) custom-call(f32[2,128,4,4,128]{4,3,2,1,0:T(4,128)} %psi_hbm.1, bf16[16,128,128]{2,1,0:T(8,128)(2,1)} %left_ref.1, bf16[16,128,128]{2,1,0:T(8,128)(2,1)} %right_ref.1, bf16[16,16,16]{2,1,0:T(8,128)(2,1)} %phys_ref.1), custom_call_target="tpu_custom_call" | custom-call | tf_op jit(solution)/shard_map/pallas_call | solution.py:411
  133.0 0.0 copy-start.1
  133.0 0.0 copy-start
  133.0 3.1 %copy.10 = f32[2,7,16,4,4,128]{5,4,3,2,1,0:T(4,128)} copy(f32[2,7,16,4,4,128]{5,4,3,2,1,0:T(4,128)} %get-tuple-element.6) | data formatting | bytes 3670016
  136.1 0.0 copy-done.1
  136.1 0.6 copy.11
  136.6 0.0 copy-done
  136.7 0.6 copy.12
Async XLA Ops:
  133.0 3.1 %copy-start.1 = (f32[2,6]{1,0:T(2,128)S(1)}, f32[2,6]{1,0:T(2,128)}, u32[]{:S(2)}) copy-start(f32[2,6]{1,0:T(2,128)} %get-tuple-element.7) | copy-start | bytes 148
  133.0 3.7 %copy-start = (f32[2,6]{1,0:T(2,128)S(1)}, f32[2,6]{1,0:T(2,128)}, u32[]{:S(2)}) copy-start(f32[2,6]{1,0:T(2,128)} %get-tuple-element.8) | copy-start | bytes 148

commit v9 on v8

--- a/solution.py
+++ b/solution.py
@@ -16,7 +16,6 @@
 ROWS = 16
 N_ELEMS = float(BOND * PAIRS * BOND)
 FORM_BEFORE = 0
-COLLECT_BEFORE = 4
 POST_BEFORE = 6
 MESH = pl.DeviceIdType.MESH
 F32 = jnp.float32
@@ -39,9 +38,9 @@
 
 
 def kernel(
-    psi_hbm, left_ref, right_ref, phys_ref, out_ref, alpha_ref, beta_ref,
+    psi_hbm, left_ref, right_ref, phys_ref, out_hbm, alpha_ref, beta_ref,
     left, right, phys, wide, v_in, y_buf, z_buf0, z_buf1, acc, sig, v_cur, v_prev, beta_old, stats, mine,
-    turned, got, got_end, across, numbers, dense, psi_ref, psi_sem, tri,
+    turned, got, got_end, across, numbers, dense, psi_ref, psi_sem, tri, squares, out_ref, out_sem,
     r_send, r_recv, w_send, w_recv, l_send, l_recv, s_send, s_recv, g_send, g_recv, o_send, o_recv, e_send, e_recv,
 ):
     me = lax.axis_index("terms")
@@ -87,9 +86,10 @@
         slot = v_in.at[r, peers[e], g * 8 : (g + 1) * 8]
         return copy(slot, slot, g_send.at[r, g, e + 1], g_recv.at[r, g, e + 1], 1)
 
-    def o_copy(r, e):
+    def o_copy(r, j, e):
         rows = pl.ds(pl.multiple_of(peers[e] * ROWS, ROWS), ROWS)
-        return copy(turned.at[r, :, rows, :], got.at[r, me], o_send.at[r, e], o_recv.at[r, e], e)
+        way = lax.rem(j, 2)
+        return copy(turned.at[r, :, rows, :], got.at[r, way, me], o_send.at[r, way, e], o_recv.at[r, way, e], e)
 
     def e_copy(e):
         rows = pl.ds(pl.multiple_of(peers[e] * ROWS, ROWS), ROWS)
@@ -141,21 +141,18 @@
     beta_old[...] = jnp.zeros_like(beta_old)
     numbers[...] = jnp.zeros_like(numbers)
 
-    for psi_copy in psi_copies:
-        psi_copy.wait()
-
-    @pl.loop(0, 2)
-    def _(r):
-        acc[0:BOND, :] = jnp.zeros((BOND, BOND), F32)
+    def prepare(r):
+        psi_copies[r].wait()
+        squares[...] = jnp.zeros((BOND, BOND), F32)
 
         @pl.loop(0, 4)
         def _(s):
             for t in range(4):
                 x = psi_ref[r, :, s, t, :]
-                acc[0:BOND, :] += x * x
+                squares[...] += x * x
                 across[s * 4 + t] = x.T
 
-        norm = jnp.sqrt(total(acc[0:BOND, :]) / N_ELEMS)
+        norm = jnp.sqrt(total(squares[...]) / N_ELEMS)
 
         @pl.loop(0, PAIRS)
         def _(u):
@@ -166,6 +163,8 @@
             v_cur[r, pl.ds(row + BOND, 8), :] = two[8:16]
 
         out_ref[r, 0] = psi_ref[r, own] / norm.reshape(1, 1, 1, 1)
+
+    prepare(0)
 
     sub = lax.broadcasted_iota(jnp.int32, (8, BOND), 0)
     lane = lax.broadcasted_iota(jnp.int32, (8, BOND), 1)
@@ -260,16 +259,15 @@
 
         turn(r, joined)
 
-    def post(r):
+    def post(r, j):
         for e in (6, 7, 2, 3, 4, 5, 1):
-            o_copy(r, e).start()
-        got[r, me] = turned[r, :, own, :]
-
-    def relay(r):
-        for g in range(2):
-            for e in (4, 6, 2):
-                g_copy(r, g, e).wait()
-                g_pass(r, g, e).start()
+            o_copy(r, j, e).start()
+        got[r, lax.rem(j, 2), me] = turned[r, :, own, :]
+
+    def relay(r, g):
+        for e in (4, 6, 2):
+            g_copy(r, g, e).wait()
+            g_pass(r, g, e).start()
 
     def arrive(r, g):
         g_copy(r, g, 1).wait()
@@ -294,8 +292,8 @@
 
     def collect(r, j):
         for e in range(1, DEVS):
-            o_copy(r, e).wait()
-        for q, x in enumerate(assemble(lambda p, g: got[r, p, g])):
+            o_copy(r, j, e).wait()
+        for q, x in enumerate(assemble(lambda p, g: got[r, lax.rem(j, 2), p, g])):
             out_ref[r, j + 1, :, q // 4, q % 4, :] = x
 
     acc[...] = jnp.zeros_like(acc)
@@ -321,6 +319,7 @@
 
         @pl.when(d == 2)
         def _():
+            prepare(1)
             for e, x in ((2, 0), (4, 1)):
                 l_copy(e, x).wait()
                 l_far(x).start()
@@ -368,21 +367,23 @@
         for d in range(DEVS):
             if d == FORM_BEFORE:
                 advance(pr, pj, t == 2 * STEPS - 1)
-            if d == COLLECT_BEFORE:
-
-                @pl.when(t >= 2)
-                def _():
-                    collect(r, j - 1)
-
             if d == POST_BEFORE:
-                post(pr)
+                post(pr, pj)
             form_out(d, (z_buf0, z_buf1)[d % 2], d == 0)
 
         share(r)
 
         @pl.when(t < 2 * STEPS - 1)
         def _():
-            relay(pr)
+            relay(pr, 0)
+
+        @pl.when(t >= 2)
+        def _():
+            collect(r, j - 1)
+
+        @pl.when(t < 2 * STEPS - 1)
+        def _():
+            relay(pr, 1)
 
     halves = sig[1].reshape(2, PAIRS, 8, BOND)
     turn(1, jnp.concatenate([halves[0], halves[1]], axis=1))
@@ -390,6 +391,10 @@
         e_copy(e).start()
     got_end[me] = turned[1, :, own, :]
     collect(0, STEPS - 1)
+    done = [(slice(0, 1), slice(0, STEPS + 1)), (slice(1, 2), slice(0, STEPS)), (slice(1, 2), slice(STEPS, STEPS + 1))]
+    writes = [pltpu.make_async_copy(out_ref.at[x, y], out_hbm.at[x, y], out_sem.at[i]) for i, (x, y) in enumerate(done)]
+    writes[0].start()
+    writes[1].start()
     alpha, beta = scalars(1, STEPS - 1)
     shift = jnp.zeros((1, BOND), F32)
     for p in range(DEVS):
@@ -399,6 +404,9 @@
     for q, x in enumerate(assemble(lambda p, g: got_end[p, g])):
         v = out_ref[1, STEPS - 1, :, q // 4, q % 4, :]
         out_ref[1, STEPS, :, q // 4, q % 4, :] = (x - shift * v) / beta
+    writes[2].start()
+    for write in writes:
+        write.wait()
     alpha_ref[...] = numbers[0, 0:2, 0:STEPS]
     beta_ref[...] = numbers[1, 0:2, 0:STEPS]
 
@@ -416,7 +424,7 @@
                 jax.ShapeDtypeStruct((roots, STEPS), F32),
             ),
             in_specs=[pl.BlockSpec(memory_space=pl.ANY), vm, vm, vm],
-            out_specs=(vm, vm, vm),
+            out_specs=(pl.BlockSpec(memory_space=pl.ANY), vm, vm),
             scratch_shapes=[
                 pltpu.VMEM((DEVS, TERMS, BOND, BOND), BF16),
                 pltpu.VMEM((DEVS, TERMS, ROWS, BOND), BF16),
@@ -434,7 +442,7 @@
                 pltpu.VMEM((roots, DEVS, 8, BOND), F32),
                 pltpu.VMEM((roots, 8, BOND), F32),
                 pltpu.VMEM((roots, 2, BOND, BOND), F32),
-                pltpu.VMEM((roots, DEVS, 2, ROWS, BOND), F32),
+                pltpu.VMEM((roots, 2, DEVS, 2, ROWS, BOND), F32),
                 pltpu.VMEM((DEVS, 2, ROWS, BOND), F32),
                 pltpu.VMEM((PAIRS, BOND, BOND), F32),
                 pltpu.VMEM((2, 8, BOND), F32),
@@ -442,9 +450,12 @@
                 pltpu.VMEM(psi.shape, F32),
                 dma((roots,)),
                 pltpu.VMEM((DEVS, PACKED, BOND), BF16),
+                pltpu.VMEM((BOND, BOND), F32),
+                pltpu.VMEM((roots, STEPS + 1, ROWS) + psi.shape[2:], F32),
+                dma((3,)),
                 dma((DEVS,)), dma((DEVS,)), dma((DEVS,)), dma((DEVS,)), dma((DEVS, 2)), dma((DEVS, 2)),
                 dma((roots, DEVS)), dma((roots, DEVS)), dma((roots, 2, DEVS)), dma((roots, 2, DEVS)),
-                dma((roots, DEVS)), dma((roots, DEVS)), dma((DEVS,)), dma((DEVS,)),
+                dma((roots, 2, DEVS)), dma((roots, 2, DEVS)), dma((DEVS,)), dma((DEVS,)),
             ],
             compiler_params=pltpu.CompilerParams(
                 collective_id=0, has_side_effects=True, vmem_limit_bytes=56 * 1024 * 1024

time: 137 us -> 132 us (0.964)
  Pallas kernels: 132 us -> 127 us
    pallas_call x1, Pallas kernels: 132 us -> 127 us  [device_fn(): pl.pallas_call(kernel, out_shape=(jax.ShapeDtypeStruct((roots, STEPS + 1,...]
where the time goes in v9:
time: 132 us
  Pallas kernels  127 us (96%)
  local copies, waits for them, and re-layouts  4.23 us (3%)
    pallas_call x1, Pallas kernels, device_fn(): pl.pallas_call(kernel, out_shape=(jax.ShapeDtypeStruct((roots, STEPS + 1,...  127 us
    unnamed x7, local copies, waits for them, and re-layouts  4.23 us

profile of v9, /device:TPU:0, one launch (start us, length us, event | category | flops | bytes accessed | tf_op | source)
XLA Modules:
  0.0 132.2 jit_solution(9933024695856402603)
XLA Ops:
  0.6 127.3 %shard_map.67 = (f32[2,7,16,4,4,128]{5,4,3,2,1,0:T(4,128)}, f32[2,6]{1,0:T(2,128)}, f32[2,6]{1,0:T(2,128)}) custom-call(f32[2,128,4,4,128]{4,3,2,1,0:T(4,128)} %psi_hbm.1, bf16[16,128,128]{2,1,0:T(8,128)(2,1)} %left_ref.1, bf16[16,128,128]{2,1,0:T(8,128)(2,1)} %right_ref.1, bf16[16,16,16]{2,1,0:T(8,128)(2,1)} %phys_ref.1), custom_call_target="tpu_custom_call" | custom-call | tf_op jit(solution)/shard_map/pallas_call | solution.py:419
  128.0 0.0 copy-start.1
  128.0 0.0 copy-start
  128.0 3.1 %copy.10 = f32[2,7,16,4,4,128]{5,4,3,2,1,0:T(4,128)} copy(f32[2,7,16,4,4,128]{5,4,3,2,1,0:T(4,128)} %get-tuple-element.6) | data formatting | bytes 3670016
  131.1 0.0 copy-done.1
  131.1 0.6 copy.11
  131.7 0.0 copy-done
  131.7 0.6 copy.12
Async XLA Ops:
  128.0 3.1 %copy-start.1 = (f32[2,6]{1,0:T(2,128)S(1)}, f32[2,6]{1,0:T(2,128)}, u32[]{:S(2)}) copy-start(f32[2,6]{1,0:T(2,128)} %get-tuple-element.7) | copy-start | bytes 148
  128.0 3.7 %copy-start = (f32[2,6]{1,0:T(2,128)S(1)}, f32[2,6]{1,0:T(2,128)}, u32[]{:S(2)}) copy-start(f32[2,6]{1,0:T(2,128)} %get-tuple-element.8) | copy-start | bytes 148

commit v10 on v9

--- a/solution.py
+++ b/solution.py
@@ -16,7 +16,6 @@
 ROWS = 16
 N_ELEMS = float(BOND * PAIRS * BOND)
 FORM_BEFORE = 0
-POST_BEFORE = 6
 MESH = pl.DeviceIdType.MESH
 F32 = jnp.float32
 BF16 = jnp.bfloat16
@@ -38,17 +37,25 @@
 
 
 def kernel(
-    psi_hbm, left_ref, right_ref, phys_ref, out_hbm, alpha_ref, beta_ref,
+    psi_hbm, left_hbm, right_hbm, phys_hbm, out_hbm, alpha_ref, beta_ref,
     left, right, phys, wide, v_in, y_buf, z_buf0, z_buf1, acc, sig, v_cur, v_prev, beta_old, stats, mine,
     turned, got, got_end, across, numbers, dense, psi_ref, psi_sem, tri, squares, out_ref, out_sem,
+    left_ref, right_ref, phys_ref, in_sem,
     r_send, r_recv, w_send, w_recv, l_send, l_recv, s_send, s_recv, g_send, g_recv, o_send, o_recv, e_send, e_recv,
 ):
     me = lax.axis_index("terms")
     peers = {e: flip(me, e) for e in range(1, DEVS)}
 
+    pairs = ((right_hbm, right_ref), (phys_hbm, phys_ref), (left_hbm, left_ref))
+    in_copies = [pltpu.make_async_copy(src, dst, in_sem.at[i]) for i, (src, dst) in enumerate(pairs)]
     psi_copies = [pltpu.make_async_copy(psi_hbm.at[r], psi_ref.at[r], psi_sem.at[r]) for r in range(2)]
-    for psi_copy in psi_copies:
-        psi_copy.start()
+    for in_copy in in_copies + psi_copies:
+        in_copy.start()
+    barrier = pltpu.get_barrier_semaphore()
+    for e in range(1, DEVS):
+        pl.semaphore_signal(barrier, inc=1, device_id=(peers[e],), device_id_type=MESH)
+    for in_copy in in_copies:
+        in_copy.wait()
 
     def copy(src, dst, send, recv, e):
         return pltpu.make_async_remote_copy(
@@ -123,9 +130,6 @@
         put = jnp.where(col_qu == row_u + q * PAIRS, 1.0, 0.0).astype(BF16)
         flat += jnp.dot(w_own[:, q, :].astype(BF16), put, preferred_element_type=F32)
     dense[...] = flat.astype(BF16)
-    barrier = pltpu.get_barrier_semaphore()
-    for e in range(1, DEVS):
-        pl.semaphore_signal(barrier, inc=1, device_id=(peers[e],), device_id_type=MESH)
     pl.semaphore_wait(barrier, DEVS - 1)
 
     for e in (1, 2, 4, 3, 5, 6, 7):
@@ -257,9 +261,10 @@
                 for e in (6, 4, 2, 1):
                     g_copy(r, g, e).start()
 
-        turn(r, joined)
 
     def post(r, j):
+        halves = v_cur[r].reshape(2, PAIRS, 8, BOND)
+        turn(r, jnp.concatenate([halves[0], halves[1]], axis=1))
         for e in (6, 7, 2, 3, 4, 5, 1):
             o_copy(r, j, e).start()
         got[r, lax.rem(j, 2), me] = turned[r, :, own, :]
@@ -319,11 +324,11 @@
 
         @pl.when(d == 2)
         def _():
-            prepare(1)
             for e, x in ((2, 0), (4, 1)):
                 l_copy(e, x).wait()
                 l_far(x).start()
                 l_pass(e, x).start()
+            prepare(1)
             for e, x in ((2, 1), (4, 0)):
                 l_copy(e, x).wait()
                 l_pass(e, x).start()
@@ -367,8 +372,11 @@
         for d in range(DEVS):
             if d == FORM_BEFORE:
                 advance(pr, pj, t == 2 * STEPS - 1)
-            if d == POST_BEFORE:
-                post(pr, pj)
+
+                @pl.when(t == 2 * STEPS - 1)
+                def _():
+                    post(pr, pj)
+
             form_out(d, (z_buf0, z_buf1)[d % 2], d == 0)
 
         share(r)
@@ -376,6 +384,7 @@
         @pl.when(t < 2 * STEPS - 1)
         def _():
             relay(pr, 0)
+            post(pr, pj)
 
         @pl.when(t >= 2)
         def _():
@@ -423,7 +432,7 @@
                 jax.ShapeDtypeStruct((roots, STEPS), F32),
                 jax.ShapeDtypeStruct((roots, STEPS), F32),
             ),
-            in_specs=[pl.BlockSpec(memory_space=pl.ANY), vm, vm, vm],
+            in_specs=[pl.BlockSpec(memory_space=pl.ANY)] * 4,
             out_specs=(pl.BlockSpec(memory_space=pl.ANY), vm, vm),
             scratch_shapes=[
                 pltpu.VMEM((DEVS, TERMS, BOND, BOND), BF16),
@@ -453,6 +462,10 @@
                 pltpu.VMEM((BOND, BOND), F32),
                 pltpu.VMEM((roots, STEPS + 1, ROWS) + psi.shape[2:], F32),
                 dma((3,)),
+                pltpu.VMEM((TERMS, BOND, BOND), BF16),
+                pltpu.VMEM((TERMS, BOND, BOND), BF16),
+                pltpu.VMEM((TERMS, PAIRS, PAIRS), BF16),
+                dma((3,)),
                 dma((DEVS,)), dma((DEVS,)), dma((DEVS,)), dma((DEVS,)), dma((DEVS, 2)), dma((DEVS, 2)),
                 dma((roots, DEVS)), dma((roots, DEVS)), dma((roots, 2, DEVS)), dma((roots, 2, DEVS)),
                 dma((roots, 2, DEVS)), dma((roots, 2, DEVS)), dma((DEVS,)), dma((DEVS,)),

time: 132 us -> 130 us (0.985)
  Pallas kernels: 127 us -> 125 us
    pallas_call x1, Pallas kernels: 127 us -> 125 us  [device_fn(): pl.pallas_call(kernel, out_shape=(jax.ShapeDtypeStruct((roots, STEPS + 1,...]
where the time goes in v10:
time: 130 us
  Pallas kernels  125 us (96%)
  local copies, waits for them, and re-layouts  4.23 us (3%)
    pallas_call x1, Pallas kernels, device_fn(): pl.pallas_call(kernel, out_shape=(jax.ShapeDtypeStruct((roots, STEPS + 1,...  125 us
    unnamed x7, local copies, waits for them, and re-layouts  4.23 us

profile of v10, /device:TPU:0, one launch (start us, length us, event | category | flops | bytes accessed | tf_op | source)
XLA Modules:
  0.0 129.9 jit_solution(16536079169722856171)
XLA Ops:
  0.6 125.0 %shard_map.67 = (f32[2,7,16,4,4,128]{5,4,3,2,1,0:T(4,128)}, f32[2,6]{1,0:T(2,128)}, f32[2,6]{1,0:T(2,128)}) custom-call(f32[2,128,4,4,128]{4,3,2,1,0:T(4,128)} %psi_hbm.1, bf16[16,128,128]{2,1,0:T(8,128)(2,1)} %left_hbm.1, bf16[16,128,128]{2,1,0:T(8,128)(2,1)} %right_hbm.1, bf16[16,16,16]{2,1,0:T(8,128)(2,1)} %phys_hbm.1), custom_call_target="tpu_custom_call" | custom-call | tf_op jit(solution)/shard_map/pallas_call | solution.py:428
  125.6 0.0 copy-start.1
  125.6 0.0 copy-start
  125.6 3.1 %copy.10 = f32[2,7,16,4,4,128]{5,4,3,2,1,0:T(4,128)} copy(f32[2,7,16,4,4,128]{5,4,3,2,1,0:T(4,128)} %get-tuple-element.6) | data formatting | bytes 3670016
  128.7 0.0 copy-done.1
  128.7 0.6 copy.11
  129.3 0.0 copy-done
  129.3 0.6 copy.12
Async XLA Ops:
  125.6 3.1 %copy-start.1 = (f32[2,6]{1,0:T(2,128)S(1)}, f32[2,6]{1,0:T(2,128)}, u32[]{:S(2)}) copy-start(f32[2,6]{1,0:T(2,128)} %get-tuple-element.7) | copy-start | bytes 148
  125.6 3.7 %copy-start = (f32[2,6]{1,0:T(2,128)S(1)}, f32[2,6]{1,0:T(2,128)}, u32[]{:S(2)}) copy-start(f32[2,6]{1,0:T(2,128)} %get-tuple-element.8) | copy-start | bytes 148

commit v11 on v10

--- a/solution.py
+++ b/solution.py
@@ -37,10 +37,10 @@
 
 
 def kernel(
-    psi_hbm, left_hbm, right_hbm, phys_hbm, out_hbm, alpha_ref, beta_ref,
+    psi_hbm, left_hbm, right_hbm, phys_hbm, out_hbm, alpha_hbm, beta_hbm, scale_hbm,
     left, right, phys, wide, v_in, y_buf, z_buf0, z_buf1, acc, sig, v_cur, v_prev, beta_old, stats, mine,
     turned, got, got_end, across, numbers, dense, psi_ref, psi_sem, tri, squares, out_ref, out_sem,
-    left_ref, right_ref, phys_ref, in_sem,
+    left_ref, right_ref, phys_ref, in_sem, alpha_ref, beta_ref, scale_ref,
     r_send, r_recv, w_send, w_recv, l_send, l_recv, s_send, s_recv, g_send, g_recv, o_send, o_recv, e_send, e_recv,
 ):
     me = lax.axis_index("terms")
@@ -166,7 +166,8 @@
             v_cur[r, pl.ds(row, 8), :] = two[0:8]
             v_cur[r, pl.ds(row + BOND, 8), :] = two[8:16]
 
-        out_ref[r, 0] = psi_ref[r, own] / norm.reshape(1, 1, 1, 1)
+        for q in range(PAIRS):
+            out_ref[r, 0, :, q, :] = psi_ref[r, own, q // 4, q % 4, :] / norm
 
     prepare(0)
 
@@ -299,9 +300,8 @@
         for e in range(1, DEVS):
             o_copy(r, j, e).wait()
         for q, x in enumerate(assemble(lambda p, g: got[r, lax.rem(j, 2), p, g])):
-            out_ref[r, j + 1, :, q // 4, q % 4, :] = x
-
-    acc[...] = jnp.zeros_like(acc)
+            out_ref[r, j + 1, :, q, :] = x
+
 
     @pl.loop(0, DEVS)
     def _(d):
@@ -315,15 +315,12 @@
         widen(d)
         form_y(0, d, range(0, PAIRS, 2))
 
-    @pl.loop(0, DEVS)
-    def _(d):
-        @pl.when(d == 1)
-        def _():
+    for d in range(DEVS):
+        nxt = d + 1
+        if nxt == 1:
             l_copy(1, 0).wait()
             l_copy(1, 1).wait()
-
-        @pl.when(d == 2)
-        def _():
+        elif nxt == 2:
             for e, x in ((2, 0), (4, 1)):
                 l_copy(e, x).wait()
                 l_far(x).start()
@@ -332,25 +329,16 @@
             for e, x in ((2, 1), (4, 0)):
                 l_copy(e, x).wait()
                 l_pass(e, x).start()
-
-        @pl.when(d == 6)
-        def _():
+        elif nxt == 6:
             for x in range(2):
                 l_far(x).wait()
                 l_pass(6, x).start()
-
-        for e in (3, 5, 7):
-
-            @pl.when(d == e)
-            def _():
-                for x in range(2):
-                    l_pass(e - 1, x).wait()
-
-        @pl.when(d >= 1)
-        def _():
-            unpack(d)
-
-        form_out(d, z_buf0, False)
+        elif nxt in (3, 5, 7):
+            for x in range(2):
+                l_pass(nxt - 1, x).wait()
+        if nxt < DEVS:
+            unpack(nxt)
+        form_out(d, (z_buf0, z_buf1)[d % 2], d == 0)
 
     share(0)
 
@@ -411,29 +399,36 @@
     for e in range(1, DEVS):
         e_copy(e).wait()
     for q, x in enumerate(assemble(lambda p, g: got_end[p, g])):
-        v = out_ref[1, STEPS - 1, :, q // 4, q % 4, :]
-        out_ref[1, STEPS, :, q // 4, q % 4, :] = (x - shift * v) / beta
-    writes[2].start()
+        v = out_ref[1, STEPS - 1, :, q, :]
+        out_ref[1, STEPS, :, q, :] = x - shift * v
+    alpha_ref[...] = numbers[0, 0:2, 0:STEPS]
+    beta_ref[...] = numbers[1, 0:2, 0:STEPS]
+    end = jnp.logical_and(sub == 1, lane == STEPS)
+    scale_ref[...] = jnp.where(end, 1.0 / beta, jnp.ones((8, BOND), F32))[0:2, 0 : STEPS + 1]
+    writes.append(pltpu.make_async_copy(scale_ref, scale_hbm, out_sem.at[5]))
+    writes.append(pltpu.make_async_copy(alpha_ref, alpha_hbm, out_sem.at[3]))
+    writes.append(pltpu.make_async_copy(beta_ref, beta_hbm, out_sem.at[4]))
+    for write in writes[2:]:
+        write.start()
     for write in writes:
         write.wait()
-    alpha_ref[...] = numbers[0, 0:2, 0:STEPS]
-    beta_ref[...] = numbers[1, 0:2, 0:STEPS]
 
 
 def solution(mesh):
     def device_fn(psi, left_loc, phys_loc, right_loc):
         roots = psi.shape[0]
-        vm = pl.BlockSpec(memory_space=pltpu.VMEM)
+        anywhere = pl.BlockSpec(memory_space=pl.ANY)
         dma = pltpu.SemaphoreType.DMA
-        return pl.pallas_call(
+        vecs, alpha, beta, scale = pl.pallas_call(
             kernel,
             out_shape=(
-                jax.ShapeDtypeStruct((roots, STEPS + 1, ROWS) + psi.shape[2:], F32),
+                jax.ShapeDtypeStruct((roots, STEPS + 1, ROWS, PAIRS, BOND), F32),
                 jax.ShapeDtypeStruct((roots, STEPS), F32),
                 jax.ShapeDtypeStruct((roots, STEPS), F32),
+                jax.ShapeDtypeStruct((roots, STEPS + 1), F32),
             ),
-            in_specs=[pl.BlockSpec(memory_space=pl.ANY)] * 4,
-            out_specs=(pl.BlockSpec(memory_space=pl.ANY), vm, vm),
+            in_specs=[anywhere] * 4,
+            out_specs=[anywhere] * 4,
             scratch_shapes=[
                 pltpu.VMEM((DEVS, TERMS, BOND, BOND), BF16),
                 pltpu.VMEM((DEVS, TERMS, ROWS, BOND), BF16),
@@ -460,12 +455,15 @@
                 dma((roots,)),
                 pltpu.VMEM((DEVS, PACKED, BOND), BF16),
                 pltpu.VMEM((BOND, BOND), F32),
-                pltpu.VMEM((roots, STEPS + 1, ROWS) + psi.shape[2:], F32),
-                dma((3,)),
+                pltpu.VMEM((roots, STEPS + 1, ROWS, PAIRS, BOND), F32),
+                dma((6,)),
                 pltpu.VMEM((TERMS, BOND, BOND), BF16),
                 pltpu.VMEM((TERMS, BOND, BOND), BF16),
                 pltpu.VMEM((TERMS, PAIRS, PAIRS), BF16),
                 dma((3,)),
+                pltpu.VMEM((roots, STEPS), F32),
+                pltpu.VMEM((roots, STEPS), F32),
+                pltpu.VMEM((roots, STEPS + 1), F32),
                 dma((DEVS,)), dma((DEVS,)), dma((DEVS,)), dma((DEVS,)), dma((DEVS, 2)), dma((DEVS, 2)),
                 dma((roots, DEVS)), dma((roots, DEVS)), dma((roots, 2, DEVS)), dma((roots, 2, DEVS)),
                 dma((roots, 2, DEVS)), dma((roots, 2, DEVS)), dma((DEVS,)), dma((DEVS,)),
@@ -474,6 +472,8 @@
                 collective_id=0, has_side_effects=True, vmem_limit_bytes=56 * 1024 * 1024
             ),
         )(psi, left_loc, right_loc, phys_loc)
+        vecs = vecs * scale[:, :, None, None, None]
+        return vecs.reshape(roots, STEPS + 1, ROWS, *psi.shape[2:]), alpha, beta
 
     return jax.shard_map(
         device_fn, mesh=mesh, in_specs=(P(), P("terms"), P("terms"), P("terms")),

time: 130 us -> 129 us (level)
  local copies, waits for them, and re-layouts: 4.23 us -> 1.13 us
  other arithmetic: 0 us -> 3 us
    unnamed x7 -> x6, local copies, waits for them, and re-layouts: 4.23 us -> 1.13 us
    mul x0 -> x1, other arithmetic: none -> 3 us  [device_fn(): vecs = vecs * scale[:, :, None, None, None]]
where the time goes in v11:
time: 129 us
  Pallas kernels  124 us (96%)
  other arithmetic  3 us (2%)
    pallas_call x1, Pallas kernels, device_fn(): pl.pallas_call(kernel, out_shape=(jax.ShapeDtypeStruct((roots, STEPS + 1,...  124 us
    mul x1, other arithmetic, device_fn(): vecs = vecs * scale[:, :, None, None, None]  3 us

profile of v11, /device:TPU:0, one launch (start us, length us, event | category | flops | bytes accessed | tf_op | source)
XLA Modules:
  0.0 128.9 jit_solution(4984231084567983073)
XLA Ops:
  0.6 124.1 %shard_map.67 = (f32[2,7,16,16,128]{4,3,2,1,0:T(8,128)}, f32[2,6]{1,0:T(2,128)}, f32[2,6]{1,0:T(2,128)}, f32[2,7]{1,0:T(2,128)}) custom-call(f32[2,128,4,4,128]{4,3,2,1,0:T(4,128)} %psi_hbm.1, bf16[16,128,128]{2,1,0:T(8,128)(2,1)} %left_hbm.1, bf16[16,128,128]{2,1,0:T(8,128)(2,1)} %right_hbm.1, bf16[16,16,16]{2,1,0:T(8,128)(2,1)} %phys_hbm.1), custom_call_target="tpu_custom_call" | custom-call | tf_op jit(solution)/shard_map/pallas_call | solution.py:422
  124.7 0.0 copy-start.1
  124.8 0.0 copy-start
  124.8 3.0 %broadcast_multiply_fusion = f32[2,7,16,16,128]{4,3,2,1,0:T(8,128)} fusion(f32[2,7,16,16,128]{4,3,2,1,0:T(8,128)} %get-tuple-element.7, f32[2,7]{1,0:T(2,128)} %get-tuple-element.8), kind=kLoop, calls=%fused_computation | loop fusion | flops 458752 | bytes 3670072 | tf_op jit(solution)/shard_map/mul | solution.py:475
  127.8 0.0 copy-done.1
  127.8 0.6 copy.9
  128.3 0.0 copy-done
  128.3 0.6 copy.10
Async XLA Ops:
  124.7 3.0 %copy-start.1 = (f32[2,6]{1,0:T(2,128)S(1)}, f32[2,6]{1,0:T(2,128)}, u32[]{:S(2)}) copy-start(f32[2,6]{1,0:T(2,128)} %get-tuple-element.15) | copy-start | bytes 148
  124.8 3.6 %copy-start = (f32[2,6]{1,0:T(2,128)S(1)}, f32[2,6]{1,0:T(2,128)}, u32[]{:S(2)}) copy-start(f32[2,6]{1,0:T(2,128)} %get-tuple-element.16) | copy-start | bytes 148

commit v12 on v11

--- a/solution.py
+++ b/solution.py
@@ -37,25 +37,20 @@
 
 
 def kernel(
-    psi_hbm, left_hbm, right_hbm, phys_hbm, out_hbm, alpha_hbm, beta_hbm, scale_hbm,
+    psi_hbm, left_ref, right_ref, phys_ref, out_ref, alpha_ref, beta_ref, scale_ref,
     left, right, phys, wide, v_in, y_buf, z_buf0, z_buf1, acc, sig, v_cur, v_prev, beta_old, stats, mine,
-    turned, got, got_end, across, numbers, dense, psi_ref, psi_sem, tri, squares, out_ref, out_sem,
-    left_ref, right_ref, phys_ref, in_sem, alpha_ref, beta_ref, scale_ref,
+    turned, got, got_end, across, numbers, dense, psi_ref, psi_sem, tri, squares,
     r_send, r_recv, w_send, w_recv, l_send, l_recv, s_send, s_recv, g_send, g_recv, o_send, o_recv, e_send, e_recv,
 ):
     me = lax.axis_index("terms")
     peers = {e: flip(me, e) for e in range(1, DEVS)}
 
-    pairs = ((right_hbm, right_ref), (phys_hbm, phys_ref), (left_hbm, left_ref))
-    in_copies = [pltpu.make_async_copy(src, dst, in_sem.at[i]) for i, (src, dst) in enumerate(pairs)]
     psi_copies = [pltpu.make_async_copy(psi_hbm.at[r], psi_ref.at[r], psi_sem.at[r]) for r in range(2)]
-    for in_copy in in_copies + psi_copies:
-        in_copy.start()
+    for psi_copy in psi_copies:
+        psi_copy.start()
     barrier = pltpu.get_barrier_semaphore()
     for e in range(1, DEVS):
         pl.semaphore_signal(barrier, inc=1, device_id=(peers[e],), device_id_type=MESH)
-    for in_copy in in_copies:
-        in_copy.wait()
 
     def copy(src, dst, send, recv, e):
         return pltpu.make_async_remote_copy(
@@ -388,10 +383,6 @@
         e_copy(e).start()
     got_end[me] = turned[1, :, own, :]
     collect(0, STEPS - 1)
-    done = [(slice(0, 1), slice(0, STEPS + 1)), (slice(1, 2), slice(0, STEPS)), (slice(1, 2), slice(STEPS, STEPS + 1))]
-    writes = [pltpu.make_async_copy(out_ref.at[x, y], out_hbm.at[x, y], out_sem.at[i]) for i, (x, y) in enumerate(done)]
-    writes[0].start()
-    writes[1].start()
     alpha, beta = scalars(1, STEPS - 1)
     shift = jnp.zeros((1, BOND), F32)
     for p in range(DEVS):
@@ -405,19 +396,12 @@
     beta_ref[...] = numbers[1, 0:2, 0:STEPS]
     end = jnp.logical_and(sub == 1, lane == STEPS)
     scale_ref[...] = jnp.where(end, 1.0 / beta, jnp.ones((8, BOND), F32))[0:2, 0 : STEPS + 1]
-    writes.append(pltpu.make_async_copy(scale_ref, scale_hbm, out_sem.at[5]))
-    writes.append(pltpu.make_async_copy(alpha_ref, alpha_hbm, out_sem.at[3]))
-    writes.append(pltpu.make_async_copy(beta_ref, beta_hbm, out_sem.at[4]))
-    for write in writes[2:]:
-        write.start()
-    for write in writes:
-        write.wait()
 
 
 def solution(mesh):
     def device_fn(psi, left_loc, phys_loc, right_loc):
         roots = psi.shape[0]
-        anywhere = pl.BlockSpec(memory_space=pl.ANY)
+        anywhere, vm = pl.BlockSpec(memory_space=pl.ANY), pl.BlockSpec(memory_space=pltpu.VMEM)
         dma = pltpu.SemaphoreType.DMA
         vecs, alpha, beta, scale = pl.pallas_call(
             kernel,
@@ -427,8 +411,8 @@
                 jax.ShapeDtypeStruct((roots, STEPS), F32),
                 jax.ShapeDtypeStruct((roots, STEPS + 1), F32),
             ),
-            in_specs=[anywhere] * 4,
-            out_specs=[anywhere] * 4,
+            in_specs=[anywhere, vm, vm, vm],
+            out_specs=[vm] * 4,
             scratch_shapes=[
                 pltpu.VMEM((DEVS, TERMS, BOND, BOND), BF16),
                 pltpu.VMEM((DEVS, TERMS, ROWS, BOND), BF16),
@@ -455,21 +439,12 @@
                 dma((roots,)),
                 pltpu.VMEM((DEVS, PACKED, BOND), BF16),
                 pltpu.VMEM((BOND, BOND), F32),
-                pltpu.VMEM((roots, STEPS + 1, ROWS, PAIRS, BOND), F32),
-                dma((6,)),
-                pltpu.VMEM((TERMS, BOND, BOND), BF16),
-                pltpu.VMEM((TERMS, BOND, BOND), BF16),
-                pltpu.VMEM((TERMS, PAIRS, PAIRS), BF16),
-                dma((3,)),
-                pltpu.VMEM((roots, STEPS), F32),
-                pltpu.VMEM((roots, STEPS), F32),
-                pltpu.VMEM((roots, STEPS + 1), F32),
                 dma((DEVS,)), dma((DEVS,)), dma((DEVS,)), dma((DEVS,)), dma((DEVS, 2)), dma((DEVS, 2)),
                 dma((roots, DEVS)), dma((roots, DEVS)), dma((roots, 2, DEVS)), dma((roots, 2, DEVS)),
                 dma((roots, 2, DEVS)), dma((roots, 2, DEVS)), dma((DEVS,)), dma((DEVS,)),
             ],
             compiler_params=pltpu.CompilerParams(
-                collective_id=0, has_side_effects=True, vmem_limit_bytes=56 * 1024 * 1024
+                collective_id=0, has_side_effects=True, vmem_limit_bytes=50 * 1024 * 1024
             ),
         )(psi, left_loc, right_loc, phys_loc)
         vecs = vecs * scale[:, :, None, None, None]

time: 129 us -> 129 us (level)
  local copies, waits for them, and re-layouts: 1.13 us -> 4.04 us
  other arithmetic: 3 us -> 1.5 us
    unnamed x6 -> x8, local copies, waits for them, and re-layouts: 1.13 us -> 4.04 us
    mul x1, other arithmetic: 3 us -> 1.5 us  [device_fn(): vecs = vecs * scale[:, :, None, None, None]]
where the time goes in v12:
time: 129 us
  Pallas kernels  123 us (95%)
  local copies, waits for them, and re-layouts  4.04 us (3%)
  other arithmetic  1.5 us (1%)
    pallas_call x1, Pallas kernels, device_fn(): pl.pallas_call(kernel, out_shape=(jax.ShapeDtypeStruct((roots, STEPS + 1,...  123 us
    unnamed x8, local copies, waits for them, and re-layouts  4.04 us

profile of v12, /device:TPU:0, one launch (start us, length us, event | category | flops | bytes accessed | tf_op | source)
XLA Modules:
  0.0 129.2 jit_solution(11087960796395254337)
XLA Ops:
  0.6 0.0 copy-start
  0.6 1.0 copy-done
  1.7 0.0 copy-start.1
  1.7 1.0 copy-done.1
  2.7 0.0 copy-start.2
  2.7 0.8 copy-done.2
  3.6 123.0 %shard_map.67 = (f32[2,7,16,16,128]{4,3,2,1,0:T(8,128)S(1)}, f32[2,6]{1,0:T(2,128)S(1)}, f32[2,6]{1,0:T(2,128)S(1)}, f32[2,7]{1,0:T(2,128)S(1)}) custom-call(f32[2,128,4,4,128]{4,3,2,1,0:T(4,128)} %psi_hbm.1, bf16[16,128,128]{2,1,0:T(8,128)(2,1)S(1)} %copy-done, bf16[16,128,128]{2,1,0:T(8,128)(2,1)S(1)} %copy-done.1, bf16[16,16,16]{2,1,0:T(8,128)(2,1)S(1)} %copy-done.2), custom_call_target="tpu_custom_call" | custom-call | tf_op jit(solution)/shard_map/pallas_call | solution.py:406
  126.5 1.5 %broadcast_multiply_fusion = f32[2,7,16,16,128]{4,3,2,1,0:T(8,128)} fusion(f32[2,7,16,16,128]{4,3,2,1,0:T(8,128)S(1)} %get-tuple-element.7, f32[2,7]{1,0:T(2,128)S(1)} %get-tuple-element.8), kind=kLoop, calls=%fused_computation | loop fusion | flops 458752 | bytes 3670072 | tf_op jit(solution)/shard_map/mul | solution.py:450
  128.0 0.6 copy.9
  128.6 0.6 copy.10
Async XLA Ops:
  0.6 1.0 copy-start
  1.7 1.0 copy-start.1
  2.7 0.8 copy-start.2

commit v13 on v12

--- a/solution.py
+++ b/solution.py
@@ -37,20 +37,25 @@
 
 
 def kernel(
-    psi_hbm, left_ref, right_ref, phys_ref, out_ref, alpha_ref, beta_ref, scale_ref,
+    psi_hbm, left_hbm, right_hbm, phys_hbm, out_ref, alpha_ref, beta_ref, scale_ref,
     left, right, phys, wide, v_in, y_buf, z_buf0, z_buf1, acc, sig, v_cur, v_prev, beta_old, stats, mine,
     turned, got, got_end, across, numbers, dense, psi_ref, psi_sem, tri, squares,
+    left_ref, right_ref, phys_ref, in_sem,
     r_send, r_recv, w_send, w_recv, l_send, l_recv, s_send, s_recv, g_send, g_recv, o_send, o_recv, e_send, e_recv,
 ):
     me = lax.axis_index("terms")
     peers = {e: flip(me, e) for e in range(1, DEVS)}
 
+    pairs = ((right_hbm, right_ref), (phys_hbm, phys_ref), (left_hbm, left_ref))
+    in_copies = [pltpu.make_async_copy(src, dst, in_sem.at[i]) for i, (src, dst) in enumerate(pairs)]
     psi_copies = [pltpu.make_async_copy(psi_hbm.at[r], psi_ref.at[r], psi_sem.at[r]) for r in range(2)]
-    for psi_copy in psi_copies:
-        psi_copy.start()
+    for in_copy in in_copies + psi_copies:
+        in_copy.start()
     barrier = pltpu.get_barrier_semaphore()
     for e in range(1, DEVS):
         pl.semaphore_signal(barrier, inc=1, device_id=(peers[e],), device_id_type=MESH)
+    for in_copy in in_copies:
+        in_copy.wait()
 
     def copy(src, dst, send, recv, e):
         return pltpu.make_async_remote_copy(
@@ -401,7 +406,6 @@
 def solution(mesh):
     def device_fn(psi, left_loc, phys_loc, right_loc):
         roots = psi.shape[0]
-        anywhere, vm = pl.BlockSpec(memory_space=pl.ANY), pl.BlockSpec(memory_space=pltpu.VMEM)
         dma = pltpu.SemaphoreType.DMA
         vecs, alpha, beta, scale = pl.pallas_call(
             kernel,
@@ -411,8 +415,8 @@
                 jax.ShapeDtypeStruct((roots, STEPS), F32),
                 jax.ShapeDtypeStruct((roots, STEPS + 1), F32),
             ),
-            in_specs=[anywhere, vm, vm, vm],
-            out_specs=[vm] * 4,
+            in_specs=[pl.BlockSpec(memory_space=pltpu.HBM)] * 4,
+            out_specs=[pl.BlockSpec(memory_space=pltpu.VMEM)] * 4,
             scratch_shapes=[
                 pltpu.VMEM((DEVS, TERMS, BOND, BOND), BF16),
                 pltpu.VMEM((DEVS, TERMS, ROWS, BOND), BF16),
@@ -439,6 +443,10 @@
                 dma((roots,)),
                 pltpu.VMEM((DEVS, PACKED, BOND), BF16),
                 pltpu.VMEM((BOND, BOND), F32),
+                pltpu.VMEM((TERMS, BOND, BOND), BF16),
+                pltpu.VMEM((TERMS, BOND, BOND), BF16),
+                pltpu.VMEM((TERMS, PAIRS, PAIRS), BF16),
+                dma((3,)),
                 dma((DEVS,)), dma((DEVS,)), dma((DEVS,)), dma((DEVS,)), dma((DEVS, 2)), dma((DEVS, 2)),
                 dma((roots, DEVS)), dma((roots, DEVS)), dma((roots, 2, DEVS)), dma((roots, 2, DEVS)),
                 dma((roots, 2, DEVS)), dma((roots, 2, DEVS)), dma((DEVS,)), dma((DEVS,)),
@@ -446,7 +454,7 @@
             compiler_params=pltpu.CompilerParams(
                 collective_id=0, has_side_effects=True, vmem_limit_bytes=50 * 1024 * 1024
             ),
-        )(psi, left_loc, right_loc, phys_loc)
+        )(*[pltpu.with_memory_space_constraint(x, pltpu.HBM) for x in (psi, left_loc, right_loc, phys_loc)])
         vecs = vecs * scale[:, :, None, None, None]
         return vecs.reshape(roots, STEPS + 1, ROWS, *psi.shape[2:]), alpha, beta
 

time: 129 us -> 127 us (0.984)
  local copies, waits for them, and re-layouts: 4.04 us -> 1.12 us
    unnamed x8 -> x2, local copies, waits for them, and re-layouts: 4.04 us -> 1.12 us
where the time goes in v13:
time: 127 us
  Pallas kernels  123 us (97%)
  other arithmetic  1.5 us (1%)
    pallas_call x1, Pallas kernels, device_fn(): pl.pallas_call(kernel, out_shape=(jax.ShapeDtypeStruct((roots, STEPS + 1,...  123 us

profile of v13, /device:TPU:0, one launch (start us, length us, event | category | flops | bytes accessed | tf_op | source)
XLA Modules:
  0.0 126.7 jit_solution(8654067719107874848)
XLA Ops:
  0.6 123.4 %shard_map.67 = (f32[2,7,16,16,128]{4,3,2,1,0:T(8,128)S(1)}, f32[2,6]{1,0:T(2,128)S(1)}, f32[2,6]{1,0:T(2,128)S(1)}, f32[2,7]{1,0:T(2,128)S(1)}) custom-call(f32[2,128,4,4,128]{4,3,2,1,0:T(4,128)} %psi_hbm.1, bf16[16,128,128]{2,1,0:T(8,128)(2,1)} %left_hbm.1, bf16[16,128,128]{2,1,0:T(8,128)(2,1)} %right_hbm.1, bf16[16,16,16]{2,1,0:T(8,128)(2,1)} %phys_hbm.1), custom_call_target="tpu_custom_call" | custom-call | tf_op jit(solution)/shard_map/pallas_call | solution.py:410
  124.0 1.5 %broadcast_multiply_fusion = f32[2,7,16,16,128]{4,3,2,1,0:T(8,128)} fusion(f32[2,7,16,16,128]{4,3,2,1,0:T(8,128)S(1)} %get-tuple-element.7, f32[2,7]{1,0:T(2,128)S(1)} %get-tuple-element.8), kind=kLoop, calls=%fused_computation | loop fusion | flops 458752 | bytes 3670072 | tf_op jit(solution)/shard_map/mul | solution.py:458
  125.5 0.6 copy.9
  126.1 0.6 copy.10

commit v14 on v13

--- a/solution.py
+++ b/solution.py
@@ -37,7 +37,7 @@
 
 
 def kernel(
-    psi_hbm, left_hbm, right_hbm, phys_hbm, out_ref, alpha_ref, beta_ref, scale_ref,
+    psi_hbm, left_hbm, right_hbm, phys_hbm, out_ref, number_ref, scale_ref,
     left, right, phys, wide, v_in, y_buf, z_buf0, z_buf1, acc, sig, v_cur, v_prev, beta_old, stats, mine,
     turned, got, got_end, across, numbers, dense, psi_ref, psi_sem, tri, squares,
     left_ref, right_ref, phys_ref, in_sem,
@@ -397,8 +397,7 @@
     for q, x in enumerate(assemble(lambda p, g: got_end[p, g])):
         v = out_ref[1, STEPS - 1, :, q, :]
         out_ref[1, STEPS, :, q, :] = x - shift * v
-    alpha_ref[...] = numbers[0, 0:2, 0:STEPS]
-    beta_ref[...] = numbers[1, 0:2, 0:STEPS]
+    number_ref[...] = numbers[...]
     end = jnp.logical_and(sub == 1, lane == STEPS)
     scale_ref[...] = jnp.where(end, 1.0 / beta, jnp.ones((8, BOND), F32))[0:2, 0 : STEPS + 1]
 
@@ -407,16 +406,15 @@
     def device_fn(psi, left_loc, phys_loc, right_loc):
         roots = psi.shape[0]
         dma = pltpu.SemaphoreType.DMA
-        vecs, alpha, beta, scale = pl.pallas_call(
+        vecs, both, scale = pl.pallas_call(
             kernel,
             out_shape=(
                 jax.ShapeDtypeStruct((roots, STEPS + 1, ROWS, PAIRS, BOND), F32),
-                jax.ShapeDtypeStruct((roots, STEPS), F32),
-                jax.ShapeDtypeStruct((roots, STEPS), F32),
+                jax.ShapeDtypeStruct((2, 8, BOND), F32),
                 jax.ShapeDtypeStruct((roots, STEPS + 1), F32),
             ),
             in_specs=[pl.BlockSpec(memory_space=pltpu.HBM)] * 4,
-            out_specs=[pl.BlockSpec(memory_space=pltpu.VMEM)] * 4,
+            out_specs=[pl.BlockSpec(memory_space=pltpu.VMEM)] * 3,
             scratch_shapes=[
                 pltpu.VMEM((DEVS, TERMS, BOND, BOND), BF16),
                 pltpu.VMEM((DEVS, TERMS, ROWS, BOND), BF16),
@@ -456,7 +454,7 @@
             ),
         )(*[pltpu.with_memory_space_constraint(x, pltpu.HBM) for x in (psi, left_loc, right_loc, phys_loc)])
         vecs = vecs * scale[:, :, None, None, None]
-        return vecs.reshape(roots, STEPS + 1, ROWS, *psi.shape[2:]), alpha, beta
+        return vecs.reshape(roots, STEPS + 1, ROWS, *psi.shape[2:]), both[0, :roots, :STEPS], both[1, :roots, :STEPS]
 
     return jax.shard_map(
         device_fn, mesh=mesh, in_specs=(P(), P("terms"), P("terms"), P("terms")),

time: 127 us -> 126 us (level)
  no operation moved by 1% of the time
where the time goes in v14:
time: 126 us
  Pallas kernels  123 us (98%)
  other arithmetic  1.5 us (1%)
    pallas_call x1, Pallas kernels, device_fn(): pl.pallas_call(kernel, out_shape=(jax.ShapeDtypeStruct((roots, STEPS + 1,...  123 us

profile of v14, /device:TPU:0, one launch (start us, length us, event | category | flops | bytes accessed | tf_op | source)
XLA Modules:
  0.0 126.1 jit_solution(2711948069009028085)
XLA Ops:
  0.6 123.4 %shard_map.67 = (f32[2,7,16,16,128]{4,3,2,1,0:T(8,128)S(1)}, f32[2,8,128]{2,1,0:T(8,128)S(1)}, f32[2,7]{1,0:T(2,128)S(1)}) custom-call(f32[2,128,4,4,128]{4,3,2,1,0:T(4,128)} %psi_hbm.1, bf16[16,128,128]{2,1,0:T(8,128)(2,1)} %left_hbm.1, bf16[16,128,128]{2,1,0:T(8,128)(2,1)} %right_hbm.1, bf16[16,16,16]{2,1,0:T(8,128)(2,1)} %phys_hbm.1), custom_call_target="tpu_custom_call" | custom-call | tf_op jit(solution)/shard_map/pallas_call | solution.py:409
  124.0 1.5 %broadcast_multiply_fusion = f32[2,7,16,16,128]{4,3,2,1,0:T(8,128)} fusion(f32[2,7,16,16,128]{4,3,2,1,0:T(8,128)S(1)} %get-tuple-element.6, f32[2,7]{1,0:T(2,128)S(1)} %get-tuple-element.7), kind=kLoop, calls=%fused_computation | loop fusion | flops 458752 | bytes 3670072 | tf_op jit(solution)/shard_map/mul | solution.py:456
  125.5 0.6 slice_bitcast_fusion

commit v15 on v14

--- a/solution.py
+++ b/solution.py
@@ -37,7 +37,7 @@
 
 
 def kernel(
-    psi_hbm, left_hbm, right_hbm, phys_hbm, out_ref, number_ref, scale_ref,
+    psi_hbm, left_hbm, right_hbm, phys_hbm, out_ref, number_ref,
     left, right, phys, wide, v_in, y_buf, z_buf0, z_buf1, acc, sig, v_cur, v_prev, beta_old, stats, mine,
     turned, got, got_end, across, numbers, dense, psi_ref, psi_sem, tri, squares,
     left_ref, right_ref, phys_ref, in_sem,
@@ -396,25 +396,22 @@
         e_copy(e).wait()
     for q, x in enumerate(assemble(lambda p, g: got_end[p, g])):
         v = out_ref[1, STEPS - 1, :, q, :]
-        out_ref[1, STEPS, :, q, :] = x - shift * v
+        out_ref[1, STEPS, :, q, :] = (x - shift * v) / beta
     number_ref[...] = numbers[...]
-    end = jnp.logical_and(sub == 1, lane == STEPS)
-    scale_ref[...] = jnp.where(end, 1.0 / beta, jnp.ones((8, BOND), F32))[0:2, 0 : STEPS + 1]
 
 
 def solution(mesh):
     def device_fn(psi, left_loc, phys_loc, right_loc):
         roots = psi.shape[0]
         dma = pltpu.SemaphoreType.DMA
-        vecs, both, scale = pl.pallas_call(
+        vecs, both = pl.pallas_call(
             kernel,
             out_shape=(
                 jax.ShapeDtypeStruct((roots, STEPS + 1, ROWS, PAIRS, BOND), F32),
                 jax.ShapeDtypeStruct((2, 8, BOND), F32),
-                jax.ShapeDtypeStruct((roots, STEPS + 1), F32),
             ),
             in_specs=[pl.BlockSpec(memory_space=pltpu.HBM)] * 4,
-            out_specs=[pl.BlockSpec(memory_space=pltpu.VMEM)] * 3,
+            out_specs=[pl.BlockSpec(memory_space=pltpu.VMEM)] * 2,
             scratch_shapes=[
                 pltpu.VMEM((DEVS, TERMS, BOND, BOND), BF16),
                 pltpu.VMEM((DEVS, TERMS, ROWS, BOND), BF16),
@@ -453,7 +450,6 @@
                 collective_id=0, has_side_effects=True, vmem_limit_bytes=50 * 1024 * 1024
             ),
         )(*[pltpu.with_memory_space_constraint(x, pltpu.HBM) for x in (psi, left_loc, right_loc, phys_loc)])
-        vecs = vecs * scale[:, :, None, None, None]
         return vecs.reshape(roots, STEPS + 1, ROWS, *psi.shape[2:]), both[0, :roots, :STEPS], both[1, :roots, :STEPS]
 
     return jax.shard_map(

time: 126 us -> 126 us (level)
  other arithmetic: 1.5 us -> 0 us
    mul x1 -> x0, other arithmetic: 1.5 us -> none  [device_fn(): vecs = vecs * scale[:, :, None, None, None]]
where the time goes in v15:
time: 126 us
  Pallas kernels  123 us (98%)
  local copies, waits for them, and re-layouts  1.8 us (1%)
    pallas_call x1, Pallas kernels, device_fn(): pl.pallas_call(kernel, out_shape=(jax.ShapeDtypeStruct((roots, STEPS + 1,...  123 us

profile of v15, /device:TPU:0, one launch (start us, length us, event | category | flops | bytes accessed | tf_op | source)
XLA Modules:
  0.0 125.8 jit_solution(1095687580259848191)
XLA Ops:
  0.6 123.4 %shard_map.67 = (f32[2,7,16,16,128]{4,3,2,1,0:T(8,128)S(1)}, f32[2,8,128]{2,1,0:T(8,128)S(1)}) custom-call(f32[2,128,4,4,128]{4,3,2,1,0:T(4,128)} %psi_hbm.1, bf16[16,128,128]{2,1,0:T(8,128)(2,1)} %left_hbm.1, bf16[16,128,128]{2,1,0:T(8,128)(2,1)} %right_hbm.1, bf16[16,16,16]{2,1,0:T(8,128)(2,1)} %phys_hbm.1), custom_call_target="tpu_custom_call" | custom-call | tf_op jit(solution)/shard_map/pallas_call | solution.py:407
  124.0 0.6 slice_bitcast_fusion
  124.6 1.2 copy.8
